TPU v7x, 32 devices: a whole 2x2x4 slice. The times are simulated.
32 devices in a mesh: gx: 2 (over x), gy: 4 (over z), gz: 4 (over y, core).
Axes of the slice: x: 2, y: 2, z: 4, core: 2. Of those that a mesh axis runs over, the one named last changes fastest.
Arguments:
- populations: float32 [39, 16, 96, 512], P(None, 'gx', 'gy', 'gz'), may hold values from 0.5 to 1.5
- relax: float32 [16, 96, 512], P('gx', 'gy', 'gz'), may hold values from 0.6 to 1.9
Outputs:
- advanced: float32 [39, 16, 96, 512], P(None, 'gx', 'gy', 'gz')
All inputs are finite; a program needn't handle non-finite values.
Results may differ from a plain program's by a relative error of at most 0.0001.
Values sent between devices are 32-bit elements; how exact they have to be, the bound alone decides.
A program may use at most 128 MiB of HBM per device.

v0:
```python
import math

import jax
import jax.numpy as jnp
from jax import lax
from jax.experimental import pallas as pl
from jax.experimental.pallas import tpu as pltpu
from jax.sharding import PartitionSpec as P

MESH = pl.DeviceIdType.MESH
AXES = ("gx", "gy", "gz")
PX = 3
PY = 8
GROUP = 32


def lattice():
    speeds = [(0, 0, 0)]
    weights = [1.0 / 12.0]
    for axis in range(3):
        for sign in (1, -1):
            vector = [0, 0, 0]
            vector[axis] = sign
            speeds.append(tuple(vector))
            weights.append(1.0 / 12.0)
    for first in (1, -1):
        for second in (1, -1):
            for third in (1, -1):
                speeds.append((first, second, third))
                weights.append(1.0 / 27.0)
    for axis in range(3):
        for sign in (2, -2):
            vector = [0, 0, 0]
            vector[axis] = sign
            speeds.append(tuple(vector))
            weights.append(2.0 / 135.0)
    for couple in ((0, 1), (0, 2), (1, 2)):
        for first in (2, -2):
            for second in (2, -2):
                vector = [0, 0, 0]
                vector[couple[0]] = first
                vector[couple[1]] = second
                speeds.append(tuple(vector))
                weights.append(1.0 / 432.0)
    for axis in range(3):
        for sign in (3, -3):
            vector = [0, 0, 0]
            vector[axis] = sign
            speeds.append(tuple(vector))
            weights.append(1.0 / 1620.0)
    return (speeds, weights)


SPEEDS, WEIGHTS = lattice()
Q = len(SPEEDS)
SQUARES = [sum(v * v for v in c) for c in SPEEDS]
PAIRS = [
    (m, SPEEDS.index(tuple(-v for v in SPEEDS[m])))
    for m in range(1, Q)
    if m < SPEEDS.index(tuple(-v for v in SPEEDS[m]))
]


def offsets(axis, sign, keep):
    rows, start = [], 0
    for m, c in enumerate(SPEEDS):
        count = c[axis] * sign
        if count > 0 and keep(c):
            rows.append((m, start, count))
            start += count
    return rows


ZCOLS = [offsets(2, sign, lambda c: True) for sign in (1, -1)]
Y1ROWS = [offsets(1, sign, lambda c: c[2] == 0) for sign in (1, -1)]
Y2ROWS = [offsets(1, sign, lambda c: c[2] != 0) for sign in (1, -1)]
Y1SIZE, Y2SIZE = 16, 8

XPURE = [[(SPEEDS.index((s * k, 0, 0)), 1, k) for s in (1, -1)] for k in (1, 2, 3)]
XZ = [(SPEEDS.index((s * 2, 0, 2)), 2, 2) for s in (1, -1)]
XY = [[(SPEEDS.index((s * 2, k, 0)), 1, 2) for s in (1, -1)] for k in (2, -2)]
XYZ = [[(SPEEDS.index((s, k, 1)), 2, 1) for s in (1, -1)] for k in (1, -1)]


def add_all(terms):
    total = terms[0]
    for term in terms[1:]:
        total = total + term
    return total


def collide(load, rate, emit):
    sums = {k: [] for k in (1, 3, 4, 8, 9)}
    flows = {k: [[], [], []] for k in (1, 3, 4, 8, 9)}
    for m, o in PAIRS:
        up, down = load(m), load(o)
        k = SQUARES[m]
        sums[k].append(up + down)
        diff = up - down
        for axis in range(3):
            if SPEEDS[m][axis] > 0:
                flows[k][axis].append((1, diff))
            elif SPEEDS[m][axis] < 0:
                flows[k][axis].append((-1, diff))
    weight = {SQUARES[m]: WEIGHTS[m] for m in range(Q)}
    size = {1: 1, 3: 1, 4: 2, 8: 2, 9: 3}
    rest = load(0)
    groups = {k: add_all(sums[k]) for k in sums}
    rho = weight[0] * rest
    energy = None
    for k in sums:
        part = weight[k] * groups[k]
        rho = rho + part
        part = part if k == 1 else float(k) * part
        energy = part if energy is None else energy + part
    flux = []
    for axis in range(3):
        total = None
        for k in flows:
            part = None
            for sign, diff in flows[k][axis]:
                if part is None:
                    part = diff if sign > 0 else -diff
                else:
                    part = part + diff if sign > 0 else part - diff
            part = (weight[k] * size[k]) * part
            total = part if total is None else total + part
        flux.append(total)
    inverse = 1.0 / rho
    velocity = [part * inverse for part in flux]
    norm = velocity[0] * velocity[0] + velocity[1] * velocity[1] + velocity[2] * velocity[2]
    t = (energy * inverse - norm) * 0.5 - 1.0
    b = 1.5 * norm
    w = [1.5 * part for part in velocity]
    keep = 1.0 - rate
    k0 = rho * rate
    k24 = k0 * (1.0 / 24.0)
    k6 = k0 * (1.0 / 6.0)
    half_b = 0.5 * b
    kt = k0 * t
    ktb = kt * b
    ktt = kt * t
    base = k0 * (1.0 - half_b + 0.5 * half_b * half_b)
    base1 = k0 * (0.5 - 0.5 * half_b)
    baseo = k0 * (1.0 - half_b)

    def even0(s):
        return (
            base
            + kt * (0.5 * (s - 3.0))
            + ktb * (0.25 * (5.0 - s))
            + ktt * ((s * s - 10.0 * s + 15.0) / 8.0)
        )

    emit(0, keep * rest + even0(0.0))
    for k in sums:
        s = 1.5 * k
        e0 = even0(s)
        e1 = base1 + kt * (0.25 * (s - 7.0))
        o1 = baseo + kt * (0.5 * (s - 5.0))
        for m, o in PAIRS:
            if SQUARES[m] != k:
                continue
            a = None
            for axis in range(3):
                v = SPEEDS[m][axis]
                if v == 0:
                    continue
                unit = w[axis]
                if a is None:
                    a = unit if v > 0 else -unit
                else:
                    a = a + unit if v > 0 else a - unit
            if size[k] != 1:
                a = float(size[k]) * a
            q = a * a
            even = e0 + q * (e1 + q * k24)
            odd = a * (o1 + q * k6)
            emit(m, keep * load(m) + (even + odd))
            emit(o, keep * load(o) + (even - odd))


def kernel(
    pop, rate, ext, g, r, zs, zr, y1s, y1r, y2s, y2r,
    in_sem, z_ss, z_rs, y1_ss, y1_rs, y2_ss, y2_rs, x_ss, x_rs,
):
    nx, ny, nz = pop.shape[1:]
    inner = nx - 4
    groups = [(0, 1), (nx - 1, 1), (1, 1), (nx - 2, 1), (2, inner)]
    loads = [
        pltpu.make_async_copy(
            pop.at[:, pl.ds(first, count)], g.at[:, pl.ds(first, count)], in_sem.at[n]
        )
        for n, (first, count) in enumerate(groups)
    ]
    loads.append(pltpu.make_async_copy(rate, r, in_sem.at[5]))

    around = []
    for axis in AXES:
        n = lax.axis_size(axis)
        me = lax.axis_index(axis)
        around.append(({axis: lax.rem(me + 1, n)}, {axis: lax.rem(me + n - 1, n)}))
    barrier = pltpu.get_barrier_semaphore()
    for pair in (around[1], around[0], around[2]):
        for target in pair:
            pl.semaphore_signal(barrier, inc=1, device_id=target, device_id_type=MESH)
    for n in (5, 0, 1, 2, 3, 4):
        loads[n].start()

    lane = lax.broadcasted_iota(jnp.int32, (ny, nz), 1)

    def layer_a(j):
        return (j % 2) * (nx - 1) + (j // 2) * (1 - 2 * (j % 2))

    def layer_b(j):
        return j + 2

    def rows_at(m):
        start = PY + SPEEDS[m][1]
        return pl.ds(start, ny)

    def edge_rows(sign, count):
        return pl.ds(PY + ny, count) if sign == 0 else pl.ds(PY - count, count)

    def home_rows(sign, count):
        return pl.ds(PY, count) if sign == 0 else pl.ds(PY + ny - count, count)

    def collide_chunk(chunk, layer, first, last, packed=None):
        def step(j, packed):
            x = layer(j)
            packed = list(packed)
            mine = [jnp.zeros((ny, nz), jnp.float32), jnp.zeros((ny, nz), jnp.float32)]
            slot = [{m: (s, c) for m, s, c in ZCOLS[d]} for d in (0, 1)]

            def emit(m, value):
                cx, cy, cz = SPEEDS[m]
                if cz:
                    d = 0 if cz > 0 else 1
                    start, count = slot[d][m]
                    shift = start + count if d == 0 else start
                    moved = pltpu.roll(value, shift, 1) if shift else value
                    mask = (lane >= start) & (lane < start + count)
                    mine[d] = jnp.where(mask, moved, mine[d])
                    value = pltpu.roll(value, cz % nz, 1)
                ext[m, PX + x + cx, rows_at(m), :] = value

            collide(lambda m: g[m, x], r[x], emit)
            for d in (0, 1):
                moved = pltpu.roll(mine[d], GROUP * j, 1)
                mask = (lane >= GROUP * j) & (lane < GROUP * j + GROUP)
                packed[d] = jnp.where(mask, moved, packed[d])
            for d in (0, 1):
                for m, start, count in Y1ROWS[d]:
                    y1s[chunk, d, j, pl.ds(start, count), :] = ext[
                        m, PX + x + SPEEDS[m][0], edge_rows(d, count), :
                    ]
            return tuple(packed)

        blank = jnp.zeros((ny, nz), jnp.float32)
        return lax.fori_loop(first, last, step, packed or (blank, blank))

    def pack_z(chunk, packed):
        for d in (0, 1):
            zs[chunk, d] = packed[d]

    def settle_z(chunk, layer, steps):
        def step(j, carry):
            x = layer(j)
            for d in (0, 1):
                back = lax.rem(nz - GROUP * j, nz)
                base = pltpu.roll(zr[chunk, d], back, 1)
                for m, start, count in ZCOLS[d]:
                    shift = start if d == 0 else start + count
                    moved = pltpu.roll(base, nz - shift, 1) if shift else base
                    mask = lane < count if d == 0 else lane >= nz - count
                    where = (m, PX + x + SPEEDS[m][0], rows_at(m), slice(None))
                    ext[where] = jnp.where(mask, moved, ext[where])
            for d in (0, 1):
                for m, start, count in Y2ROWS[d]:
                    y2s[chunk, d, j, pl.ds(start, count), :] = ext[
                        m, PX + x + SPEEDS[m][0], edge_rows(d, count), :
                    ]
            return carry

        lax.fori_loop(0, steps, step, 0)

    def settle_y(chunk, layer, steps, table, received):
        def step(j, carry):
            x = layer(j)
            for d in (0, 1):
                for m, start, count in table[d]:
                    ext[m, PX + x + SPEEDS[m][0], home_rows(d, count), :] = received[
                        chunk, d, j, pl.ds(start, count), :
                    ]
            return carry

        lax.fori_loop(0, steps, step, 0)

    def send_all(axis, chunk, src, dst, ss, rs):
        copies = []
        for d in (0, 1):
            copies.append(
                pltpu.make_async_remote_copy(
                    src_ref=src.at[chunk, d],
                    dst_ref=dst.at[chunk, d],
                    send_sem=ss.at[chunk, d],
                    recv_sem=rs.at[chunk, d],
                    device_id=around[axis][d],
                    device_id_type=MESH,
                )
            )
        for copy in copies:
            copy.start()
        return copies

    xs = []
    early = [(8, ny - 8), (0, ny - 8)]
    late = [(0, 8), (ny - 8, 8)]

    def send_x(pair, rows=None):
        start, count = rows or (0, ny)
        for d in (0, 1):
            first, members, layers = pair[d]
            n = len(xs)
            out_at = PX + nx if d == 0 else PX - layers
            in_at = PX if d == 0 else PX + nx - layers
            which, rows = pl.ds(first, members), pl.ds(PY + start, count)
            copy = pltpu.make_async_remote_copy(
                src_ref=ext.at[which, pl.ds(out_at, layers), rows],
                dst_ref=ext.at[which, pl.ds(in_at, layers), rows],
                send_sem=x_ss.at[n],
                recv_sem=x_rs.at[n],
                device_id=around[0][d],
                device_id_type=MESH,
            )
            copy.start()
            xs.append(copy)

    for n in (5, 0, 1):
        loads[n].wait()
    packed = collide_chunk(0, layer_a, 0, 2)
    loads[2].wait()
    loads[3].wait()
    pack_z(0, collide_chunk(0, layer_a, 2, 4, packed))
    pl.semaphore_wait(barrier, 6)
    send_x(XPURE[0])
    send_x(XPURE[1])
    z_a = send_all(2, 0, zs, zr, z_ss, z_rs)
    y1_a = send_all(1, 0, y1s, y1r, y1_ss, y1_rs)
    for n in (0, 1):
        send_x(XY[n], early[n])
    loads[4].wait()
    pack_z(1, collide_chunk(1, layer_b, 0, inner))
    z_b = send_all(2, 1, zs, zr, z_ss, z_rs)
    y1_b = send_all(1, 1, y1s, y1r, y1_ss, y1_rs)
    send_x(XPURE[2])

    for copy in z_a:
        copy.wait_recv()
    settle_z(0, layer_a, 4)
    y2_a = send_all(1, 0, y2s, y2r, y2_ss, y2_rs)
    send_x(XZ)
    for n in (0, 1):
        send_x(XYZ[n], early[n])
    for copy in y1_a:
        copy.wait_recv()
    settle_y(0, layer_a, 4, Y1ROWS, y1r)
    for n in (0, 1):
        send_x(XY[n], late[n])
    for copy in z_b:
        copy.wait_recv()
    settle_z(1, layer_b, inner)
    y2_b = send_all(1, 1, y2s, y2r, y2_ss, y2_rs)
    for copy in y2_a:
        copy.wait_recv()
    settle_y(0, layer_a, 4, Y2ROWS, y2r)
    for n in (0, 1):
        send_x(XYZ[n], late[n])
    for copy in y1_b:
        copy.wait_recv()
    settle_y(1, layer_b, inner, Y1ROWS, y1r)
    for copy in y2_b:
        copy.wait_recv()
    settle_y(1, layer_b, inner, Y2ROWS, y2r)
    for copy in xs:
        copy.wait_recv()
    for copy in z_a + z_b + y1_a + y1_b + y2_a + y2_b + xs:
        copy.wait_send()


def crop(ext, out, sem):
    nx, ny = out.shape[1:3]
    parts = 3
    share = Q // parts
    copies = [
        pltpu.make_async_copy(
            ext.at[pl.ds(n * share, share), pl.ds(PX, nx), pl.ds(PY, ny)],
            out.at[pl.ds(n * share, share)],
            sem.at[n],
        )
        for n in range(parts)
    ]
    for copy in copies:
        copy.start()
    for copy in copies:
        copy.wait()


def per_device(populations, relax):
    nx, ny, nz = relax.shape
    steps = max(4, nx - 4)
    shape = (Q, nx + 2 * PX, ny + 2 * PY, nz)
    f32 = jnp.float32
    dma = pltpu.SemaphoreType.DMA
    any_space = pl.BlockSpec(memory_space=pl.ANY)
    room = 67043328 - 4 * math.prod(shape) - 32768
    ext = pl.pallas_call(
        kernel,
        out_shape=pltpu.VMEM(shape, f32),
        in_specs=[pl.BlockSpec(memory_space=pltpu.HBM)] * 2,
        out_specs=pl.BlockSpec(memory_space=pltpu.VMEM),
        scratch_shapes=[
            pltpu.VMEM((Q, nx, ny, nz), f32),
            pltpu.VMEM((nx, ny, nz), f32),
            pltpu.VMEM((2, 2, ny, nz), f32),
            pltpu.VMEM((2, 2, ny, nz), f32),
            pltpu.VMEM((2, 2, steps, Y1SIZE, nz), f32),
            pltpu.VMEM((2, 2, steps, Y1SIZE, nz), f32),
            pltpu.VMEM((2, 2, steps, Y2SIZE, nz), f32),
            pltpu.VMEM((2, 2, steps, Y2SIZE, nz), f32),
            dma((6,)),
            dma((2, 2)), dma((2, 2)),
            dma((2, 2)), dma((2, 2)),
            dma((2, 2)), dma((2, 2)),
            dma((24,)), dma((24,)),
        ],
        compiler_params=pltpu.CompilerParams(
            collective_id=0, has_side_effects=True, vmem_limit_bytes=room
        ),
    )(populations, relax)
    return pl.pallas_call(
        crop,
        out_shape=jax.ShapeDtypeStruct((Q, nx, ny, nz), f32),
        in_specs=[any_space],
        out_specs=any_space,
        scratch_shapes=[dma((3,))],
        compiler_params=pltpu.CompilerParams(vmem_limit_bytes=2**20),
    )(ext)


def solution(mesh):
    return jax.shard_map(
        per_device,
        mesh=mesh,
        in_specs=(P(None, "gx", "gy", "gz"), P("gx", "gy", "gz")),
        out_specs=P(None, "gx", "gy", "gz"),
        check_vma=False,
    )
```

profile of v0, /device:TPU:0, one launch (start us, length us, event | category | flops | bytes accessed | tf_op | source)
XLA Modules:
  0.0 19.1 jit_solution(8244309094314109296)
XLA Ops:
  0.0 17.2 %shard_map.28.ext = f32[39,14,40,128]{3,2,1,0:T(8,128)S(1)} custom-call(f32[39,8,24,128]{3,2,1,0:T(8,128)} %pop.1, f32[8,24,128]{2,1,0:T(8,128)} %rate.1), custom_call_target="tpu_custom_call" | custom-call | tf_op jit(solution)/shard_map/pallas_call | solution.py:417
  17.2 1.9 %shard_map.29 = f32[39,8,24,128]{3,2,1,0:T(8,128)} custom-call(f32[39,14,40,128]{3,2,1,0:T(8,128)S(1)} %shard_map.28.ext), custom_call_target="tpu_custom_call" | custom-call | tf_op jit(solution)/shard_map/pallas_call | solution.py:441
where the time goes:
time: 19.3 us; the launch traced here: 19.1 us
  Pallas kernels  19.1 us (99%)
    pallas_call x1, Pallas kernels, per_device(): pl.pallas_call(kernel, out_shape=pltpu.VMEM(shape, f32), in_specs=[pl.Blo...  17.2 us
    pallas_call x1, Pallas kernels, per_device(): pl.pallas_call(crop, out_shape=jax.ShapeDtypeStruct((Q, nx, ny, nz), f32)...  1.92 us

commit v1 on v0

v1 whole, which is shorter than its diff:
```python
import math

import jax
import jax.numpy as jnp
from jax import lax
from jax.experimental import pallas as pl
from jax.experimental.pallas import tpu as pltpu
from jax.sharding import PartitionSpec as P

MESH = pl.DeviceIdType.MESH
AXES = ("gx", "gy", "gz")
PX = 3
PY = 8
TILE = 8


def lattice():
    speeds = [(0, 0, 0)]
    weights = [1.0 / 12.0]
    for axis in range(3):
        for sign in (1, -1):
            vector = [0, 0, 0]
            vector[axis] = sign
            speeds.append(tuple(vector))
            weights.append(1.0 / 12.0)
    for first in (1, -1):
        for second in (1, -1):
            for third in (1, -1):
                speeds.append((first, second, third))
                weights.append(1.0 / 27.0)
    for axis in range(3):
        for sign in (2, -2):
            vector = [0, 0, 0]
            vector[axis] = sign
            speeds.append(tuple(vector))
            weights.append(2.0 / 135.0)
    for couple in ((0, 1), (0, 2), (1, 2)):
        for first in (2, -2):
            for second in (2, -2):
                vector = [0, 0, 0]
                vector[couple[0]] = first
                vector[couple[1]] = second
                speeds.append(tuple(vector))
                weights.append(1.0 / 432.0)
    for axis in range(3):
        for sign in (3, -3):
            vector = [0, 0, 0]
            vector[axis] = sign
            speeds.append(tuple(vector))
            weights.append(1.0 / 1620.0)
    return (speeds, weights)


SPEEDS, WEIGHTS = lattice()
Q = len(SPEEDS)
SQUARES = [sum(v * v for v in c) for c in SPEEDS]
PAIRS = [
    (m, SPEEDS.index(tuple(-v for v in SPEEDS[m])))
    for m in range(1, Q)
    if m < SPEEDS.index(tuple(-v for v in SPEEDS[m]))
]


EDGE = [
    (m, o) for m, o in PAIRS if SPEEDS[m][2] == 0 and SPEEDS[m][0] != 0
]
REST = [pair for pair in PAIRS if pair not in EDGE]


def crossing(m, x, nx):
    at = x + SPEEDS[m][0]
    return 0 if at >= nx else 1 if at < 0 else None


def slots(axis, sign, layers, keep):
    rows, start = [], 0
    for x in layers:
        for m, c in enumerate(SPEEDS):
            count = c[axis] * sign
            if count > 0 and keep(m, x):
                rows.append((m, x, start, count))
                start += count
    return rows, start


def plan(nx):
    order = []
    for x in range((nx + 1) // 2):
        order += [x] if x == nx - 1 - x else [x, nx - 1 - x]
    chunks = [order[:2], order[2:4], order[4:]]
    zcols = [
        [slots(2, sign, layers, lambda m, x: True)[0] for sign in (1, -1)]
        for layers in chunks
    ]
    kinds = [
        lambda m, x: crossing(m, x, nx) is not None and SPEEDS[m][2] == 0,
        lambda m, x: crossing(m, x, nx) is not None and SPEEDS[m][2] != 0,
        lambda m, x: crossing(m, x, nx) is None and SPEEDS[m][2] == 0,
        lambda m, x: crossing(m, x, nx) is None and SPEEDS[m][2] != 0,
    ]
    yrows, start = [], 0
    for keep in kinds:
        both = [slots(1, sign, order, keep) for sign in (1, -1)]
        size = -(-max(n for _, n in both) // TILE) * TILE
        yrows.append(([rows for rows, _ in both], start, size))
        start += size
    return order, chunks, zcols, yrows, start


def add_all(terms):
    total = terms[0]
    for term in terms[1:]:
        total = total + term
    return total


def collide(load, rate):
    sums = {k: [] for k in (1, 3, 4, 8, 9)}
    flows = {k: [[], [], []] for k in (1, 3, 4, 8, 9)}
    for m, o in PAIRS:
        up, down = load(m), load(o)
        k = SQUARES[m]
        sums[k].append(up + down)
        diff = up - down
        for axis in range(3):
            if SPEEDS[m][axis] > 0:
                flows[k][axis].append((1, diff))
            elif SPEEDS[m][axis] < 0:
                flows[k][axis].append((-1, diff))
    weight = {SQUARES[m]: WEIGHTS[m] for m in range(Q)}
    size = {1: 1, 3: 1, 4: 2, 8: 2, 9: 3}
    rest = load(0)
    groups = {k: add_all(sums[k]) for k in sums}
    rho = weight[0] * rest
    energy = None
    for k in sums:
        part = weight[k] * groups[k]
        rho = rho + part
        part = part if k == 1 else float(k) * part
        energy = part if energy is None else energy + part
    flux = []
    for axis in range(3):
        total = None
        for k in flows:
            part = None
            for sign, diff in flows[k][axis]:
                if part is None:
                    part = diff if sign > 0 else -diff
                else:
                    part = part + diff if sign > 0 else part - diff
            part = (weight[k] * size[k]) * part
            total = part if total is None else total + part
        flux.append(total)
    inverse = 1.0 / rho
    velocity = [part * inverse for part in flux]
    norm = velocity[0] * velocity[0] + velocity[1] * velocity[1] + velocity[2] * velocity[2]
    t = (energy * inverse - norm) * 0.5 - 1.0
    b = 1.5 * norm
    w = [1.5 * part for part in velocity]
    keep = 1.0 - rate
    k0 = rho * rate
    k24 = k0 * (1.0 / 24.0)
    k6 = k0 * (1.0 / 6.0)
    half_b = 0.5 * b
    kt = k0 * t
    ktb = kt * b
    ktt = kt * t
    base = k0 * (1.0 - half_b + 0.5 * half_b * half_b)
    base1 = k0 * (0.5 - 0.5 * half_b)
    baseo = k0 * (1.0 - half_b)

    def even0(s):
        return (
            base
            + kt * (0.5 * (s - 3.0))
            + ktb * (0.25 * (5.0 - s))
            + ktt * ((s * s - 10.0 * s + 15.0) / 8.0)
        )

    def emit_rest(emit):
        emit(0, keep * rest + even0(0.0))

    def emit_pairs(pairs, emit):
        for k in sums:
            chosen = [pair for pair in pairs if SQUARES[pair[0]] == k]
            if not chosen:
                continue
            s = 1.5 * k
            e0 = even0(s)
            e1 = base1 + kt * (0.25 * (s - 7.0))
            o1 = baseo + kt * (0.5 * (s - 5.0))
            for m, o in chosen:
                a = None
                for axis in range(3):
                    v = SPEEDS[m][axis]
                    if v == 0:
                        continue
                    unit = w[axis]
                    if a is None:
                        a = unit if v > 0 else -unit
                    else:
                        a = a + unit if v > 0 else a - unit
                if size[k] != 1:
                    a = float(size[k]) * a
                q = a * a
                even = e0 + q * (e1 + q * k24)
                odd = a * (o1 + q * k6)
                emit(m, keep * load(m) + (even + odd))
                emit(o, keep * load(o) + (even - odd))

    return emit_rest, emit_pairs


def kernel(
    pop, rate, ext, g, r, zs, zr, ys, yr,
    in_sem, z_ss, z_rs, y_ss, y_rs, x_ss, x_rs, ready,
):
    nx, ny, nz = pop.shape[1:]
    order, chunks, zcols, yrows, _ = plan(nx)
    groups = [(x, 1) for x in order[:4]] + [(2, nx - 4)]
    loads = [
        pltpu.make_async_copy(
            pop.at[:, pl.ds(first, count)], g.at[:, pl.ds(first, count)], in_sem.at[n]
        )
        for n, (first, count) in enumerate(groups)
    ]
    loads.append(pltpu.make_async_copy(rate, r, in_sem.at[5]))

    around = []
    for axis in AXES:
        n = lax.axis_size(axis)
        me = lax.axis_index(axis)
        around.append(({axis: lax.rem(me + 1, n)}, {axis: lax.rem(me + n - 1, n)}))
    barrier = pltpu.get_barrier_semaphore()
    greeted = (around[1][1],) + around[0] + around[2]
    for target in greeted:
        pl.semaphore_signal(barrier, inc=1, device_id=target, device_id_type=MESH)
    for n in (5, 0, 1, 2, 3, 4):
        loads[n].start()

    lane = lax.broadcasted_iota(jnp.int32, (ny, nz), 1)

    def rows_at(m):
        return pl.ds(PY + SPEEDS[m][1], ny)

    def place(m, x):
        return PX + x + SPEEDS[m][0]

    def remote(axis, d, src, dst, ss, rs):
        return pltpu.make_async_remote_copy(
            src_ref=src, dst_ref=dst, send_sem=ss, recv_sem=rs,
            device_id=around[axis][d], device_id_type=MESH,
        )

    sent = []

    def send_x(m, members, x, rows):
        d = crossing(m, x, nx)
        at = place(m, x)
        home = at - nx if d == 0 else at + nx
        start, count = rows
        which, rows = pl.ds(m, members), pl.ds(PY + start, count)
        remote(
            0, d, ext.at[which, pl.ds(at, 1), rows], ext.at[which, pl.ds(home, 1), rows],
            x_ss.at[0], x_rs.at[0],
        ).start()
        sent.append(members * count)

    def send_z(chunk):
        for d in (0, 1):
            remote(
                2, d, zs.at[chunk, d], zr.at[chunk, d], z_ss.at[0], z_rs.at[chunk]
            ).start()

    def send_y(kinds, d):
        for kind in kinds:
            _, start, size = yrows[kind]
            rows = pl.ds(start, size)
            remote(
                1, d, ys.at[d, rows], yr.at[d, rows], y_ss.at[0],
                y_rs.at[max(kind - 1, 0)],
            ).start()

    def early(m):
        v = SPEEDS[m][1]
        return (0, ny) if v == 0 else (TILE, ny - TILE) if v > 0 else (0, ny - TILE)

    def late(m):
        return (0, TILE) if SPEEDS[m][1] > 0 else (ny - TILE, TILE)

    def outgoing(x, chosen):
        return [m for m in range(Q) if crossing(m, x, nx) is not None and chosen(SPEEDS[m])]

    def send_edge(x):
        for m in outgoing(x, lambda c: c[2] == 0):
            send_x(m, 1, x, early(m))

    def send_tilted(x):
        for m in outgoing(x, lambda c: c[2] > 0):
            send_x(m, 2, x, early(m))

    def send_late(x):
        for m in outgoing(x, lambda c: c[1] != 0 and c[2] == 0):
            send_x(m, 1, x, late(m))
        for m in outgoing(x, lambda c: c[1] != 0 and c[2] > 0):
            send_x(m, 2, x, late(m))

    def work(x, chunk, packed, between):
        slot = [{m: (s, c) for m, at, s, c in zcols[chunk][d] if at == x} for d in (0, 1)]

        def emit(m, value):
            cz = SPEEDS[m][2]
            if cz:
                d = 0 if cz > 0 else 1
                start, count = slot[d][m]
                shift = (start + count if d == 0 else start) % nz
                moved = pltpu.roll(value, shift, 1) if shift else value
                mask = (lane >= start) & (lane < start + count)
                packed[d] = jnp.where(mask, moved, packed[d])
                value = pltpu.roll(value, cz % nz, 1)
            ext[m, place(m, x), rows_at(m), :] = value

        emit_rest, emit_pairs = collide(lambda m: g[m, x], r[x])
        emit_pairs(EDGE, emit)
        between()
        emit_rest(emit)
        emit_pairs(REST, emit)

    def settle_z(chunk, chosen):
        for d in (0, 1):
            base = zr[chunk, d]
            for m, x, start, count in zcols[chunk][d]:
                if not chosen(m, x):
                    continue
                shift = (start if d == 0 else start + count) % nz
                moved = pltpu.roll(base, nz - shift, 1) if shift else base
                mask = lane < count if d == 0 else lane >= nz - count
                where = (m, place(m, x), rows_at(m), slice(None))
                ext[where] = jnp.where(mask, moved, ext[where])

    def pack_y(kind):
        tables, first, _ = yrows[kind]
        for d in (0, 1):
            for m, x, start, count in tables[d]:
                edge = PY + ny if d == 0 else PY - count
                ys[d, pl.ds(first + start, count), :] = ext[
                    m, place(m, x), pl.ds(edge, count), :
                ]

    def settle_y(kind):
        tables, first, _ = yrows[kind]
        for d in (0, 1):
            for m, x, start, count in tables[d]:
                home = PY if d == 0 else PY + ny - count
                ext[m, place(m, x), pl.ds(home, count), :] = yr[
                    d, pl.ds(first + start, count), :
                ]

    def crosses(m, x):
        return crossing(m, x, nx) is not None

    def stays(m, x):
        return crossing(m, x, nx) is None

    def greet():
        pl.semaphore_wait(barrier, len(greeted))
        pl.semaphore_signal(ready, inc=1, device_id=around[1][0], device_id_type=MESH)

    loads[5].wait()
    blank = jnp.zeros((ny, nz), jnp.float32)
    for chunk, layers in enumerate(chunks):
        packed = [blank, blank]
        for n, x in enumerate(layers):
            if chunk < 2:
                loads[2 * chunk + n].wait()
            elif n == 0:
                loads[4].wait()

            def between(x=x):
                if x == order[0]:
                    greet()
                send_edge(x)

            work(x, chunk, packed, between)
        for d in (0, 1):
            zs[chunk, d] = packed[d]
        send_z(chunk)
        if chunk == 1:
            pack_y(0)
            send_y((0,), 0)
    pack_y(2)
    send_y((2,), 0)

    def wait_z(chunk):
        remote(2, 0, zs.at[chunk], zr.at[chunk], z_ss.at[0], z_rs.at[chunk]).wait_recv()

    wait_z(0)
    settle_z(0, crosses)
    for x in chunks[0]:
        send_tilted(x)
    pack_y(1)
    send_y((1,), 0)
    wait_z(1)
    settle_z(1, crosses)
    for x in chunks[1]:
        send_tilted(x)
    pl.semaphore_wait(ready, 1)
    send_y((1, 0, 2), 1)
    settle_z(0, stays)
    settle_z(1, stays)
    wait_z(2)
    settle_z(2, stays)
    pack_y(3)
    for d in (0, 1):
        send_y((3,), d)

    def wait_y(kinds):
        first = yrows[kinds[0]][1]
        size = sum(yrows[kind][2] for kind in kinds)
        part = (slice(None), pl.ds(first, size))
        remote(
            1, 0, ys.at[part], yr.at[part], y_ss.at[0], y_rs.at[max(kinds[0] - 1, 0)]
        ).wait_recv()

    wait_y((0, 1))
    settle_y(0)
    settle_y(1)
    for x in order:
        send_late(x)
    wait_y((2,))
    settle_y(2)
    wait_y((3,))
    settle_y(3)
    units = sum(sent) // ny
    layers = max(n for n in range(1, nx + 1) if units % n == 0)
    span = ext.at[pl.ds(0, units // layers), pl.ds(0, layers), pl.ds(PY, ny)]
    everything = remote(0, 0, span, span, x_ss.at[0], x_rs.at[0])
    everything.wait_recv()
    everything.wait_send()
    remote(1, 0, ys, ys, y_ss.at[0], y_rs.at[0]).wait_send()
    remote(2, 0, zs, zs, z_ss.at[0], z_rs.at[0]).wait_send()


def crop(ext, out, sem):
    nx, ny = out.shape[1:3]
    parts = 3
    share = Q // parts
    copies = [
        pltpu.make_async_copy(
            ext.at[pl.ds(n * share, share), pl.ds(PX, nx), pl.ds(PY, ny)],
            out.at[pl.ds(n * share, share)],
            sem.at[n],
        )
        for n in range(parts)
    ]
    for copy in copies:
        copy.start()
    for copy in copies:
        copy.wait()


def per_device(populations, relax):
    nx, ny, nz = relax.shape
    shape = (Q, nx + 2 * PX, ny + 2 * PY, nz)
    height = plan(nx)[4]
    f32 = jnp.float32
    dma = pltpu.SemaphoreType.DMA
    any_space = pl.BlockSpec(memory_space=pl.ANY)
    room = 67043328 - 4 * math.prod(shape) - 32768
    ext = pl.pallas_call(
        kernel,
        out_shape=pltpu.VMEM(shape, f32),
        in_specs=[pl.BlockSpec(memory_space=pltpu.HBM)] * 2,
        out_specs=pl.BlockSpec(memory_space=pltpu.VMEM),
        scratch_shapes=[
            pltpu.VMEM((Q, nx, ny, nz), f32),
            pltpu.VMEM((nx, ny, nz), f32),
            pltpu.VMEM((3, 2, ny, nz), f32),
            pltpu.VMEM((3, 2, ny, nz), f32),
            pltpu.VMEM((2, height, nz), f32),
            pltpu.VMEM((2, height, nz), f32),
            dma((6,)),
            dma((1,)), dma((3,)),
            dma((1,)), dma((3,)),
            dma((1,)), dma((1,)),
            pltpu.SemaphoreType.REGULAR,
        ],
        compiler_params=pltpu.CompilerParams(
            collective_id=0, has_side_effects=True, vmem_limit_bytes=room
        ),
    )(populations, relax)
    return pl.pallas_call(
        crop,
        out_shape=jax.ShapeDtypeStruct((Q, nx, ny, nz), f32),
        in_specs=[any_space],
        out_specs=any_space,
        scratch_shapes=[dma((3,))],
        compiler_params=pltpu.CompilerParams(vmem_limit_bytes=2**20),
    )(ext)


def solution(mesh):
    return jax.shard_map(
        per_device,
        mesh=mesh,
        in_specs=(P(None, "gx", "gy", "gz"), P("gx", "gy", "gz")),
        out_specs=P(None, "gx", "gy", "gz"),
        check_vma=False,
    )
```

time: 19.3 us -> 17.2 us (0.89)
  Pallas kernels: 19.1 us -> 17 us
    pallas_call x1, Pallas kernels: 17.2 us -> 15.1 us  [per_device(): pl.pallas_call(kernel, out_shape=pltpu.VMEM(shape, f32), in_specs=[pl.Blo...]
where the time goes in v1:
time: 17.2 us; the launch traced here: 17 us
  Pallas kernels  17 us (99%)
    pallas_call x1, Pallas kernels, per_device(): pl.pallas_call(kernel, out_shape=pltpu.VMEM(shape, f32), in_specs=[pl.Blo...  15.1 us
    pallas_call x1, Pallas kernels, per_device(): pl.pallas_call(crop, out_shape=jax.ShapeDtypeStruct((Q, nx, ny, nz), f32)...  1.92 us

profile of v1, /device:TPU:0, one launch (start us, length us, event | category | flops | bytes accessed | tf_op | source)
XLA Modules:
  0.0 17.0 jit_solution(11342969870152099750)
XLA Ops:
  0.0 15.1 %shard_map.28.ext = f32[39,14,40,128]{3,2,1,0:T(8,128)S(1)} custom-call(f32[39,8,24,128]{3,2,1,0:T(8,128)} %pop.1, f32[8,24,128]{2,1,0:T(8,128)} %rate.1), custom_call_target="tpu_custom_call" | custom-call | tf_op jit(solution)/shard_map/pallas_call | solution.py:470
  15.1 1.9 %shard_map.29 = f32[39,8,24,128]{3,2,1,0:T(8,128)} custom-call(f32[39,14,40,128]{3,2,1,0:T(8,128)S(1)} %shard_map.28.ext), custom_call_target="tpu_custom_call" | custom-call | tf_op jit(solution)/shard_map/pallas_call | solution.py:492

commit v2 on v1

--- a/solution.py
+++ b/solution.py
@@ -92,11 +92,11 @@
         [slots(2, sign, layers, lambda m, x: True)[0] for sign in (1, -1)]
         for layers in chunks
     ]
+    near = set(order[:4])
     kinds = [
-        lambda m, x: crossing(m, x, nx) is not None and SPEEDS[m][2] == 0,
-        lambda m, x: crossing(m, x, nx) is not None and SPEEDS[m][2] != 0,
-        lambda m, x: crossing(m, x, nx) is None and SPEEDS[m][2] == 0,
-        lambda m, x: crossing(m, x, nx) is None and SPEEDS[m][2] != 0,
+        lambda m, x: crossing(m, x, nx) is not None,
+        lambda m, x: crossing(m, x, nx) is None and x in near,
+        lambda m, x: crossing(m, x, nx) is None and x not in near,
     ]
     yrows, start = [], 0
     for keep in kinds:
@@ -212,8 +212,8 @@
 
 
 def kernel(
-    pop, rate, ext, g, r, zs, zr, ys, yr,
-    in_sem, z_ss, z_rs, y_ss, y_rs, x_ss, x_rs, ready,
+    pop, rate, ext, g, r, zs, zr, zd, ys, yr,
+    in_sem, z_ss, z_rs, d_ss, d_rs, y_ss, y_rs, x_ss, x_rs, ready,
 ):
     nx, ny, nz = pop.shape[1:]
     order, chunks, zcols, yrows, _ = plan(nx)
@@ -226,17 +226,49 @@
     ]
     loads.append(pltpu.make_async_copy(rate, r, in_sem.at[5]))
 
-    around = []
+    around, above = [], []
     for axis in AXES:
         n = lax.axis_size(axis)
         me = lax.axis_index(axis)
-        around.append(({axis: lax.rem(me + 1, n)}, {axis: lax.rem(me + n - 1, n)}))
+        near = (lax.rem(me + 1, n), lax.rem(me + n - 1, n))
+        around.append(tuple({axis: at} for at in near))
+        above.append(tuple(jnp.where(at > me, 1, 0) for at in near))
     barrier = pltpu.get_barrier_semaphore()
-    greeted = (around[1][1],) + around[0] + around[2]
-    for target in greeted:
-        pl.semaphore_signal(barrier, inc=1, device_id=target, device_id_type=MESH)
-    for n in (5, 0, 1, 2, 3, 4):
+
+    links = [
+        (((0, d),), 0) for d in (0, 1)
+    ] + [
+        (((2, d),), 1) for d in (0, 1)
+    ] + [
+        (((1, d), (2, z))[: 1 if z is None else 2], 3 - d)
+        for d in (0, 1) for z in (None, 0, 1)
+    ]
+
+    def at(steps):
+        return {name: v for axis, d in steps for name, v in around[axis][d].items()}
+
+    def is_above(steps):
+        return above[steps[0][0]][steps[0][1]]
+
+    def signal(semaphore, steps):
+        pl.semaphore_signal(semaphore, inc=1, device_id=at(steps), device_id_type=MESH)
+
+    def wait(semaphore, amount):
+        pl.when(amount > 0)(lambda: pl.semaphore_wait(semaphore, amount))
+
+    for steps, _ in links:
+        pl.when(is_above(steps) == 1)(lambda p=steps: signal(barrier, p))
+    for n in (0, 5, 1, 2, 3, 4):
         loads[n].start()
+    wait(barrier, sum(1 - is_above(steps) for steps, _ in links))
+    for steps, flag in links:
+        pl.when(is_above(steps) == 0)(lambda p=steps, f=flag: signal(ready.at[f], p))
+
+    def await_ready(axis, d=None):
+        if axis == 1:
+            wait(ready.at[2 + d], 3 * above[1][d])
+        else:
+            wait(ready.at[axis // 2], sum(above[axis]))
 
     lane = lax.broadcasted_iota(jnp.int32, (ny, nz), 1)
 
@@ -246,10 +278,10 @@
     def place(m, x):
         return PX + x + SPEEDS[m][0]
 
-    def remote(axis, d, src, dst, ss, rs):
+    def remote(steps, src, dst, ss, rs):
         return pltpu.make_async_remote_copy(
             src_ref=src, dst_ref=dst, send_sem=ss, recv_sem=rs,
-            device_id=around[axis][d], device_id_type=MESH,
+            device_id=at(steps), device_id_type=MESH,
         )
 
     sent = []
@@ -261,7 +293,7 @@
         start, count = rows
         which, rows = pl.ds(m, members), pl.ds(PY + start, count)
         remote(
-            0, d, ext.at[which, pl.ds(at, 1), rows], ext.at[which, pl.ds(home, 1), rows],
+            ((0, d),), ext.at[which, pl.ds(at, 1), rows], ext.at[which, pl.ds(home, 1), rows],
             x_ss.at[0], x_rs.at[0],
         ).start()
         sent.append(members * count)
@@ -269,17 +301,24 @@
     def send_z(chunk):
         for d in (0, 1):
             remote(
-                2, d, zs.at[chunk, d], zr.at[chunk, d], z_ss.at[0], z_rs.at[chunk]
+                ((2, d),), zs.at[chunk, d], zr.at[chunk, d], z_ss.at[0], z_rs.at[chunk]
             ).start()
 
-    def send_y(kinds, d):
-        for kind in kinds:
-            _, start, size = yrows[kind]
-            rows = pl.ds(start, size)
+    def send_corners(first, count, d):
+        part = pl.ds(first, count)
+        rows = pl.ds(ny - TILE if d == 0 else 0, TILE)
+        for z in (0, 1):
             remote(
-                1, d, ys.at[d, rows], yr.at[d, rows], y_ss.at[0],
-                y_rs.at[max(kind - 1, 0)],
+                ((1, d), (2, z)), zs.at[part, z, rows], zd.at[d, part, z],
+                d_ss.at[0], d_rs.at[min(first, 1)],
             ).start()
+
+    def send_y(kind, d):
+        _, start, size = yrows[kind]
+        rows = pl.ds(start, size)
+        remote(
+            ((1, d),), ys.at[d, rows], yr.at[d, rows], y_ss.at[0], y_rs.at[kind]
+        ).start()
 
     def early(m):
         v = SPEEDS[m][1]
@@ -299,11 +338,9 @@
         for m in outgoing(x, lambda c: c[2] > 0):
             send_x(m, 2, x, early(m))
 
-    def send_late(x):
-        for m in outgoing(x, lambda c: c[1] != 0 and c[2] == 0):
-            send_x(m, 1, x, late(m))
-        for m in outgoing(x, lambda c: c[1] != 0 and c[2] > 0):
-            send_x(m, 2, x, late(m))
+    def send_late(x, tilted):
+        for m in outgoing(x, lambda c: c[1] != 0 and (c[2] > 0 if tilted else c[2] == 0)):
+            send_x(m, 1 + tilted, x, late(m))
 
     def work(x, chunk, packed, between):
         slot = [{m: (s, c) for m, at, s, c in zcols[chunk][d] if at == x} for d in (0, 1)]
@@ -347,14 +384,30 @@
                     m, place(m, x), pl.ds(edge, count), :
                 ]
 
-    def settle_y(kind):
+    def settle_y(kind, chosen):
         tables, first, _ = yrows[kind]
         for d in (0, 1):
             for m, x, start, count in tables[d]:
+                if not chosen(m, x):
+                    continue
                 home = PY if d == 0 else PY + ny - count
-                ext[m, place(m, x), pl.ds(home, count), :] = yr[
-                    d, pl.ds(first + start, count), :
-                ]
+                rows = yr[d, pl.ds(first + start, count), :]
+                cz = SPEEDS[m][2]
+                if cz:
+                    z = 0 if cz > 0 else 1
+                    rows = corner(d, z, m, x, rows)
+                ext[m, place(m, x), pl.ds(home, count), :] = rows
+
+    def corner(d, z, m, x, rows):
+        chunk = next(n for n, layers in enumerate(chunks) if x in layers)
+        start, width = next((s, c) for k, at, s, c in zcols[chunk][z] if (k, at) == (m, x))
+        count = abs(SPEEDS[m][1])
+        shift = (start if z == 0 else start + width) % nz
+        tile = zd[d, chunk, z]
+        moved = pltpu.roll(tile, nz - shift, 1) if shift else tile
+        moved = moved[TILE - count :] if d == 0 else moved[:count]
+        line = lane[:count]
+        return jnp.where(line < width if z == 0 else line >= nz - width, moved, rows)
 
     def crosses(m, x):
         return crossing(m, x, nx) is not None
@@ -362,11 +415,6 @@
     def stays(m, x):
         return crossing(m, x, nx) is None
 
-    def greet():
-        pl.semaphore_wait(barrier, len(greeted))
-        pl.semaphore_signal(ready, inc=1, device_id=around[1][0], device_id_type=MESH)
-
-    loads[5].wait()
     blank = jnp.zeros((ny, nz), jnp.float32)
     for chunk, layers in enumerate(chunks):
         packed = [blank, blank]
@@ -375,88 +423,108 @@
                 loads[2 * chunk + n].wait()
             elif n == 0:
                 loads[4].wait()
+            if x == order[0]:
+                loads[5].wait()
 
             def between(x=x):
                 if x == order[0]:
-                    greet()
+                    await_ready(0)
                 send_edge(x)
 
             work(x, chunk, packed, between)
         for d in (0, 1):
             zs[chunk, d] = packed[d]
-        send_z(chunk)
+        if chunk == 0:
+            await_ready(2)
+            send_z(0)
+            await_ready(1, 0)
+            send_corners(0, 1, 0)
+            pl.when(above[1][1] == 0)(lambda: send_corners(0, 1, 1))
+        else:
+            send_z(chunk)
         if chunk == 1:
             pack_y(0)
-            send_y((0,), 0)
+            send_y(0, 0)
+            pl.when(above[1][1] == 0)(lambda: send_y(0, 1))
+            pack_y(1)
+            send_y(1, 0)
+            pl.when(above[1][1] == 0)(lambda: send_y(1, 1))
     pack_y(2)
-    send_y((2,), 0)
+    send_y(2, 0)
+    send_corners(1, 2, 0)
+
+    def down_early():
+        send_y(2, 1)
+        send_corners(1, 2, 1)
+
+    pl.when(above[1][1] == 0)(down_early)
 
     def wait_z(chunk):
-        remote(2, 0, zs.at[chunk], zr.at[chunk], z_ss.at[0], z_rs.at[chunk]).wait_recv()
+        remote(((2, 0),), zs.at[chunk], zr.at[chunk], z_ss.at[0], z_rs.at[chunk]).wait_recv()
 
     wait_z(0)
     settle_z(0, crosses)
     for x in chunks[0]:
         send_tilted(x)
-    pack_y(1)
-    send_y((1,), 0)
     wait_z(1)
     settle_z(1, crosses)
     for x in chunks[1]:
         send_tilted(x)
-    pl.semaphore_wait(ready, 1)
-    send_y((1, 0, 2), 1)
+
+    def down_late():
+        await_ready(1, 1)
+        send_corners(0, 1, 1)
+        send_y(0, 1)
+        send_corners(1, 2, 1)
+        send_y(1, 1)
+        send_y(2, 1)
+
+    pl.when(above[1][1] == 1)(down_late)
     settle_z(0, stays)
     settle_z(1, stays)
+
+    def wait_y(kind):
+        _, first, size = yrows[kind]
+        part = (slice(None), pl.ds(first, size))
+        remote(((1, 0),), ys.at[part], yr.at[part], y_ss.at[0], y_rs.at[kind]).wait_recv()
+
+    def wait_corners(first, count):
+        part = zd.at[:, pl.ds(first, count)]
+        remote(((1, 0),), part, part, d_ss.at[0], d_rs.at[min(first, 1)]).wait_recv()
+
+    wait_y(0)
+    settle_y(0, lambda m, x: SPEEDS[m][2] == 0)
+    for x in order:
+        send_late(x, 0)
+    wait_corners(0, 1)
+    settle_y(0, lambda m, x: SPEEDS[m][2] != 0)
+    for x in order:
+        send_late(x, 1)
     wait_z(2)
     settle_z(2, stays)
-    pack_y(3)
-    for d in (0, 1):
-        send_y((3,), d)
-
-    def wait_y(kinds):
-        first = yrows[kinds[0]][1]
-        size = sum(yrows[kind][2] for kind in kinds)
-        part = (slice(None), pl.ds(first, size))
-        remote(
-            1, 0, ys.at[part], yr.at[part], y_ss.at[0], y_rs.at[max(kinds[0] - 1, 0)]
-        ).wait_recv()
-
-    wait_y((0, 1))
-    settle_y(0)
-    settle_y(1)
-    for x in order:
-        send_late(x)
-    wait_y((2,))
-    settle_y(2)
-    wait_y((3,))
-    settle_y(3)
+    wait_corners(1, 2)
+    wait_y(1)
+    settle_y(1, stays)
+    wait_y(2)
+    settle_y(2, stays)
     units = sum(sent) // ny
     layers = max(n for n in range(1, nx + 1) if units % n == 0)
     span = ext.at[pl.ds(0, units // layers), pl.ds(0, layers), pl.ds(PY, ny)]
-    everything = remote(0, 0, span, span, x_ss.at[0], x_rs.at[0])
+    everything = remote(((0, 0),), span, span, x_ss.at[0], x_rs.at[0])
     everything.wait_recv()
     everything.wait_send()
-    remote(1, 0, ys, ys, y_ss.at[0], y_rs.at[0]).wait_send()
-    remote(2, 0, zs, zs, z_ss.at[0], z_rs.at[0]).wait_send()
+    remote(((1, 0),), ys, ys, y_ss.at[0], y_rs.at[0]).wait_send()
+    remote(((1, 0),), zd, zd, d_ss.at[0], d_rs.at[0]).wait_send()
+    remote(((2, 0),), zs, zs, z_ss.at[0], z_rs.at[0]).wait_send()
 
 
 def crop(ext, out, sem):
     nx, ny = out.shape[1:3]
-    parts = 3
-    share = Q // parts
-    copies = [
-        pltpu.make_async_copy(
-            ext.at[pl.ds(n * share, share), pl.ds(PX, nx), pl.ds(PY, ny)],
-            out.at[pl.ds(n * share, share)],
-            sem.at[n],
-        )
-        for n in range(parts)
-    ]
-    for copy in copies:
-        copy.start()
-    for copy in copies:
-        copy.wait()
+    inside = ext.at[:, pl.ds(PX, nx), pl.ds(PY, ny)]
+    for m in range(Q):
+        for x in range(nx):
+            pltpu.make_async_copy(inside.at[m, x], out.at[m, x], sem).start()
+    pltpu.make_async_copy(inside, out, sem).wait()
 
 
 def per_device(populations, relax):
@@ -477,13 +545,15 @@
             pltpu.VMEM((nx, ny, nz), f32),
             pltpu.VMEM((3, 2, ny, nz), f32),
             pltpu.VMEM((3, 2, ny, nz), f32),
+            pltpu.VMEM((2, 3, 2, TILE, nz), f32),
             pltpu.VMEM((2, height, nz), f32),
             pltpu.VMEM((2, height, nz), f32),
             dma((6,)),
             dma((1,)), dma((3,)),
+            dma((1,)), dma((2,)),
             dma((1,)), dma((3,)),
             dma((1,)), dma((1,)),
-            pltpu.SemaphoreType.REGULAR,
+            pltpu.SemaphoreType.REGULAR((4,)),
         ],
         compiler_params=pltpu.CompilerParams(
             collective_id=0, has_side_effects=True, vmem_limit_bytes=room
@@ -494,7 +564,7 @@
         out_shape=jax.ShapeDtypeStruct((Q, nx, ny, nz), f32),
         in_specs=[any_space],
         out_specs=any_space,
-        scratch_shapes=[dma((3,))],
+        scratch_shapes=[dma],
         compiler_params=pltpu.CompilerParams(vmem_limit_bytes=2**20),
     )(ext)
 

time: 17.2 us -> 16.5 us (0.959)
  Pallas kernels: 17 us -> 16.3 us
    pallas_call x1, Pallas kernels: 15.1 us -> 14.6 us  [per_device(): pl.pallas_call(kernel, out_shape=pltpu.VMEM(shape, f32), in_specs=[pl.Blo...]
where the time goes in v2:
time: 16.5 us; the launch traced here: 16.3 us
  Pallas kernels  16.3 us (99%)
    pallas_call x1, Pallas kernels, per_device(): pl.pallas_call(kernel, out_shape=pltpu.VMEM(shape, f32), in_specs=[pl.Blo...  14.6 us
    pallas_call x1, Pallas kernels, per_device(): pl.pallas_call(crop, out_shape=jax.ShapeDtypeStruct((Q, nx, ny, nz), f32)...  1.76 us

profile of v2, /device:TPU:0, one launch (start us, length us, event | category | flops | bytes accessed | tf_op | source)
XLA Modules:
  0.0 16.3 jit_solution(8510991883165045163)
XLA Ops:
  0.0 14.6 %shard_map.28.ext = f32[39,14,40,128]{3,2,1,0:T(8,128)S(1)} custom-call(f32[39,8,24,128]{3,2,1,0:T(8,128)} %pop.1, f32[8,24,128]{2,1,0:T(8,128)} %rate.1), custom_call_target="tpu_custom_call" | custom-call | tf_op jit(solution)/shard_map/pallas_call | solution.py:538
  14.6 1.8 %shard_map.29 = f32[39,8,24,128]{3,2,1,0:T(8,128)} custom-call(f32[39,14,40,128]{3,2,1,0:T(8,128)S(1)} %shard_map.28.ext), custom_call_target="tpu_custom_call" | custom-call | tf_op jit(solution)/shard_map/pallas_call | solution.py:562

commit v3 on v2

--- a/solution.py
+++ b/solution.py
@@ -12,6 +12,7 @@
 PX = 3
 PY = 8
 TILE = 8
+FERRY = (2, 1)
 
 
 def lattice():
@@ -212,8 +213,8 @@
 
 
 def kernel(
-    pop, rate, ext, g, r, zs, zr, zd, ys, yr,
-    in_sem, z_ss, z_rs, d_ss, d_rs, y_ss, y_rs, x_ss, x_rs, ready,
+    pop, rate, ext, g, r, zs, zr, zd, ys, yr, hop,
+    in_sem, z_ss, z_rs, d_ss, d_rs, y_ss, y_rs, x_ss, x_rs, h_ss, h_rs, ready,
 ):
     nx, ny, nz = pop.shape[1:]
     order, chunks, zcols, yrows, _ = plan(nx)
@@ -226,11 +227,12 @@
     ]
     loads.append(pltpu.make_async_copy(rate, r, in_sem.at[5]))
 
-    around, above = [], []
+    around, above, nears = [], [], []
     for axis in AXES:
         n = lax.axis_size(axis)
         me = lax.axis_index(axis)
         near = (lax.rem(me + 1, n), lax.rem(me + n - 1, n))
+        nears.append(near)
         around.append(tuple({axis: at} for at in near))
         above.append(tuple(jnp.where(at > me, 1, 0) for at in near))
     barrier = pltpu.get_barrier_semaphore()
@@ -240,15 +242,28 @@
     ] + [
         (((2, d),), 1) for d in (0, 1)
     ] + [
-        (((1, d), (2, z))[: 1 if z is None else 2], 3 - d)
+        (((1, d), (2, z))[: 1 if z is None else 2], 2 + d)
         for d in (0, 1) for z in (None, 0, 1)
     ]
 
     def at(steps):
         return {name: v for axis, d in steps for name, v in around[axis][d].items()}
 
+    size = [lax.axis_size(axis) for axis in AXES]
+    me = [lax.axis_index(axis) for axis in AXES]
+    last = [jnp.where(me[1] == end, 1, 0) for end in (size[1] - 1, 0)]
+    chip = me[2] // 2
+    apart = [
+        jnp.where((n // 2 != chip) & (jnp.maximum(n, me[2]) - jnp.minimum(n, me[2]) == 1), 1, 0)
+        for n in nears[2]
+    ]
+
     def is_above(steps):
-        return above[steps[0][0]][steps[0][1]]
+        (axis, d), z = steps[0], steps[-1][1]
+        if len(steps) == 1:
+            return above[axis][d]
+        aside = (1 - last[d]) * apart[z]
+        return (1 - aside) * above[axis][d] + aside * above[2][z]
 
     def signal(semaphore, steps):
         pl.semaphore_signal(semaphore, inc=1, device_id=at(steps), device_id_type=MESH)
@@ -256,19 +271,40 @@
     def wait(semaphore, amount):
         pl.when(amount > 0)(lambda: pl.semaphore_wait(semaphore, amount))
 
+    ferry = [
+        [(SPEEDS.index((PX, 0, 0)), nx - 1 - n) for n in range(FERRY[0])],
+        [(SPEEDS.index((-PX, 0, 0)), n) for n in range(FERRY[1])],
+    ]
+    into = [jnp.where((nears[0][d] == 0) & (me[1] == 0), 1, 0) for d in (0, 1)]
+    source = [jnp.where(chip == 0, into[d], 0) for d in (0, 1)]
+    carrier = [jnp.where(chip == 1, into[d], 0) for d in (0, 1)]
+    final = jnp.where((me[0] == 0) & (me[1] == 0) & (chip == 0), 1, 0)
+    beyond = {AXES[2]: lax.rem(me[2] + 2, size[2])}
+    before = {AXES[2]: lax.rem(me[2] + size[2] - 2, size[2])}
+
+    def signal_to(semaphore, target):
+        pl.semaphore_signal(semaphore, inc=1, device_id=target, device_id_type=MESH)
+
     for steps, _ in links:
         pl.when(is_above(steps) == 1)(lambda p=steps: signal(barrier, p))
+    for d in (0, 1):
+        pl.when(source[d] == 1)(lambda: signal_to(barrier, beyond))
+        pl.when(final == 1)(lambda d=d: signal_to(barrier, {**around[0][1 - d], **beyond}))
     for n in (0, 5, 1, 2, 3, 4):
         loads[n].start()
-    wait(barrier, sum(1 - is_above(steps) for steps, _ in links))
+    wait(
+        barrier,
+        sum(1 - is_above(steps) for steps, _ in links) + 2 * (carrier[0] + carrier[1]),
+    )
     for steps, flag in links:
-        pl.when(is_above(steps) == 0)(lambda p=steps, f=flag: signal(ready.at[f], p))
+        back = 5 - flag if flag > 1 else flag
+        pl.when(is_above(steps) == 0)(lambda p=steps, f=back: signal(ready.at[f], p))
+    for d in (0, 1):
+        pl.when(carrier[d] == 1)(lambda: signal_to(ready.at[4], before))
 
     def await_ready(axis, d=None):
-        if axis == 1:
-            wait(ready.at[2 + d], 3 * above[1][d])
-        else:
-            wait(ready.at[axis // 2], sum(above[axis]))
+        flag = 2 + d if axis == 1 else axis // 2
+        wait(ready.at[flag], sum(is_above(steps) for steps, f in links if f == flag))
 
     lane = lax.broadcasted_iota(jnp.int32, (ny, nz), 1)
 
@@ -284,19 +320,53 @@
             device_id=at(steps), device_id_type=MESH,
         )
 
-    sent = []
+    def x_copy(m, members, x, rows):
+        d = crossing(m, x, nx)
+        at_x = place(m, x)
+        home = at_x - nx if d == 0 else at_x + nx
+        which, rows = pl.ds(m, members), pl.ds(PY + rows[0], rows[1])
+        return remote(
+            ((0, d),), ext.at[which, pl.ds(at_x, 1), rows], ext.at[which, pl.ds(home, 1), rows],
+            x_ss.at[0], x_rs.at[0],
+        )
 
     def send_x(m, members, x, rows):
+        copy = x_copy(m, members, x, rows)
         d = crossing(m, x, nx)
-        at = place(m, x)
-        home = at - nx if d == 0 else at + nx
-        start, count = rows
-        which, rows = pl.ds(m, members), pl.ds(PY + start, count)
-        remote(
-            ((0, d),), ext.at[which, pl.ds(at, 1), rows], ext.at[which, pl.ds(home, 1), rows],
-            x_ss.at[0], x_rs.at[0],
-        ).start()
-        sent.append(members * count)
+        if (m, x) in ferry[d]:
+            pl.when(source[d] == 0)(copy.start)
+        else:
+            copy.start()
+
+    def board(d):
+        for n, (m, x) in enumerate(ferry[d]):
+            pltpu.make_async_remote_copy(
+                src_ref=ext.at[m, place(m, x), pl.ds(PY, ny)], dst_ref=hop.at[d, n],
+                send_sem=x_ss.at[0], recv_sem=h_rs.at[d],
+                device_id=beyond, device_id_type=MESH,
+            ).start()
+
+    def carry(d):
+        span = hop.at[d, pl.ds(0, len(ferry[d]))]
+        landed = remote(((2, 0),), span, span, h_ss.at[d], h_rs.at[d])
+        landed.wait_recv()
+        for n, (m, x) in enumerate(ferry[d]):
+            at_x = place(m, x)
+            home = at_x - nx if d == 0 else at_x + nx
+            pltpu.make_async_remote_copy(
+                src_ref=hop.at[d, n], dst_ref=ext.at[m, home, pl.ds(PY, ny)],
+                send_sem=h_ss.at[d], recv_sem=x_rs.at[0],
+                device_id={**around[0][d], **before}, device_id_type=MESH,
+            ).start()
+
+    def carried(d):
+        span = hop.at[d, pl.ds(0, len(ferry[d]))]
+        remote(((2, 0),), span, span, h_ss.at[d], h_rs.at[d]).wait_send()
+
+    def ferry_when(role, act):
+        for d in (0, 1):
+            if ferry[d]:
+                pl.when(role[d] == 1)(lambda d=d: act(d))
 
     def send_z(chunk):
         for d in (0, 1):
@@ -310,7 +380,7 @@
         for z in (0, 1):
             remote(
                 ((1, d), (2, z)), zs.at[part, z, rows], zd.at[d, part, z],
-                d_ss.at[0], d_rs.at[min(first, 1)],
+                d_ss.at[0], d_rs.at[first // 2],
             ).start()
 
     def send_y(kind, d):
@@ -319,6 +389,11 @@
         remote(
             ((1, d),), ys.at[d, rows], yr.at[d, rows], y_ss.at[0], y_rs.at[kind]
         ).start()
+
+    def first_down():
+        await_ready(1, 1)
+        send_corners(0, 2, 1)
+        send_y(0, 1)
 
     def early(m):
         v = SPEEDS[m][1]
@@ -436,32 +511,25 @@
             zs[chunk, d] = packed[d]
         if chunk == 0:
             await_ready(2)
-            send_z(0)
+        send_z(chunk)
+        if chunk == 1:
+            wait(ready.at[4], source[0] + source[1])
+            ferry_when(source, board)
+            pack_y(0)
+            pack_y(1)
             await_ready(1, 0)
-            send_corners(0, 1, 0)
-            pl.when(above[1][1] == 0)(lambda: send_corners(0, 1, 1))
-        else:
-            send_z(chunk)
-        if chunk == 1:
-            pack_y(0)
+            send_corners(0, 2, 0)
             send_y(0, 0)
-            pl.when(above[1][1] == 0)(lambda: send_y(0, 1))
-            pack_y(1)
             send_y(1, 0)
-            pl.when(above[1][1] == 0)(lambda: send_y(1, 1))
+            pl.when(above[1][1] == 0)(first_down)
     pack_y(2)
     send_y(2, 0)
-    send_corners(1, 2, 0)
-
-    def down_early():
-        send_y(2, 1)
-        send_corners(1, 2, 1)
-
-    pl.when(above[1][1] == 0)(down_early)
+    send_corners(2, 1, 0)
 
     def wait_z(chunk):
         remote(((2, 0),), zs.at[chunk], zr.at[chunk], z_ss.at[0], z_rs.at[chunk]).wait_recv()
 
+    ferry_when(carrier, carry)
     wait_z(0)
     settle_z(0, crosses)
     for x in chunks[0]:
@@ -471,15 +539,10 @@
     for x in chunks[1]:
         send_tilted(x)
 
-    def down_late():
-        await_ready(1, 1)
-        send_corners(0, 1, 1)
-        send_y(0, 1)
-        send_corners(1, 2, 1)
-        send_y(1, 1)
-        send_y(2, 1)
-
-    pl.when(above[1][1] == 1)(down_late)
+    pl.when(above[1][1] == 1)(first_down)
+    send_y(1, 1)
+    send_y(2, 1)
+    send_corners(2, 1, 1)
     settle_z(0, stays)
     settle_z(1, stays)
 
@@ -490,29 +553,30 @@
 
     def wait_corners(first, count):
         part = zd.at[:, pl.ds(first, count)]
-        remote(((1, 0),), part, part, d_ss.at[0], d_rs.at[min(first, 1)]).wait_recv()
+        remote(((1, 0),), part, part, d_ss.at[0], d_rs.at[first // 2]).wait_recv()
 
     wait_y(0)
     settle_y(0, lambda m, x: SPEEDS[m][2] == 0)
     for x in order:
         send_late(x, 0)
-    wait_corners(0, 1)
+    wait_corners(0, 2)
     settle_y(0, lambda m, x: SPEEDS[m][2] != 0)
     for x in order:
         send_late(x, 1)
     wait_z(2)
     settle_z(2, stays)
-    wait_corners(1, 2)
+    wait_corners(2, 1)
     wait_y(1)
     settle_y(1, stays)
     wait_y(2)
     settle_y(2, stays)
-    units = sum(sent) // ny
+    units = sum(abs(c[0]) for c in SPEEDS)
     layers = max(n for n in range(1, nx + 1) if units % n == 0)
     span = ext.at[pl.ds(0, units // layers), pl.ds(0, layers), pl.ds(PY, ny)]
     everything = remote(((0, 0),), span, span, x_ss.at[0], x_rs.at[0])
     everything.wait_recv()
     everything.wait_send()
+    ferry_when(carrier, carried)
     remote(((1, 0),), ys, ys, y_ss.at[0], y_rs.at[0]).wait_send()
     remote(((1, 0),), zd, zd, d_ss.at[0], d_rs.at[0]).wait_send()
     remote(((2, 0),), zs, zs, z_ss.at[0], z_rs.at[0]).wait_send()
@@ -548,12 +612,14 @@
             pltpu.VMEM((2, 3, 2, TILE, nz), f32),
             pltpu.VMEM((2, height, nz), f32),
             pltpu.VMEM((2, height, nz), f32),
+            pltpu.VMEM((2, max(1, *FERRY), ny, nz), f32),
             dma((6,)),
             dma((1,)), dma((3,)),
             dma((1,)), dma((2,)),
             dma((1,)), dma((3,)),
             dma((1,)), dma((1,)),
-            pltpu.SemaphoreType.REGULAR((4,)),
+            dma((2,)), dma((2,)),
+            pltpu.SemaphoreType.REGULAR((5,)),
         ],
         compiler_params=pltpu.CompilerParams(
             collective_id=0, has_side_effects=True, vmem_limit_bytes=room

time: 16.5 us -> 16.5 us (level)
  no operation moved by 1% of the time
where the time goes in v3:
time: 16.5 us; the launch traced here: 16.3 us
  Pallas kernels  16.3 us (99%)
    pallas_call x1, Pallas kernels, per_device(): pl.pallas_call(kernel, out_shape=pltpu.VMEM(shape, f32), in_specs=[pl.Blo...  14.6 us
    pallas_call x1, Pallas kernels, per_device(): pl.pallas_call(crop, out_shape=jax.ShapeDtypeStruct((Q, nx, ny, nz), f32)...  1.76 us

profile of v3, /device:TPU:0, one launch (start us, length us, event | category | flops | bytes accessed | tf_op | source)
XLA Modules:
  0.0 16.3 jit_solution(2978583808334659345)
XLA Ops:
  0.0 14.6 %shard_map.28.ext = f32[39,14,40,128]{3,2,1,0:T(8,128)S(1)} custom-call(f32[39,8,24,128]{3,2,1,0:T(8,128)} %pop.1, f32[8,24,128]{2,1,0:T(8,128)} %rate.1), custom_call_target="tpu_custom_call" | custom-call | tf_op jit(solution)/shard_map/pallas_call | solution.py:602
  14.6 1.8 %shard_map.29 = f32[39,8,24,128]{3,2,1,0:T(8,128)} custom-call(f32[39,14,40,128]{3,2,1,0:T(8,128)S(1)} %shard_map.28.ext), custom_call_target="tpu_custom_call" | custom-call | tf_op jit(solution)/shard_map/pallas_call | solution.py:628

commit v4 on v3

--- a/solution.py
+++ b/solution.py
@@ -12,6 +12,7 @@
 PX = 3
 PY = 8
 TILE = 8
+CORNER = 2
 FERRY = (2, 1)
 
 
@@ -93,15 +94,14 @@
         [slots(2, sign, layers, lambda m, x: True)[0] for sign in (1, -1)]
         for layers in chunks
     ]
-    near = set(order[:4])
-    kinds = [
-        lambda m, x: crossing(m, x, nx) is not None,
-        lambda m, x: crossing(m, x, nx) is None and x in near,
-        lambda m, x: crossing(m, x, nx) is None and x not in near,
-    ]
+    stages = chunks[:2] + [order[4:6], order[6:]]
     yrows, start = [], 0
-    for keep in kinds:
-        both = [slots(1, sign, order, keep) for sign in (1, -1)]
+    kinds = [(order, True)] + [(layers, False) for layers in stages]
+    for layers, out in kinds:
+        both = [
+            slots(1, sign, layers, lambda m, x: (crossing(m, x, nx) is not None) == out)
+            for sign in (1, -1)
+        ]
         size = -(-max(n for _, n in both) // TILE) * TILE
         yrows.append(([rows for rows, _ in both], start, size))
         start += size
@@ -213,7 +213,7 @@
 
 
 def kernel(
-    pop, rate, ext, g, r, zs, zr, zd, ys, yr, hop,
+    pop, rate, ext, g, r, zs, zr, zc, zd, ys, yr, hop,
     in_sem, z_ss, z_rs, d_ss, d_rs, y_ss, y_rs, x_ss, x_rs, h_ss, h_rs, ready,
 ):
     nx, ny, nz = pop.shape[1:]
@@ -374,14 +374,29 @@
                 ((2, d),), zs.at[chunk, d], zr.at[chunk, d], z_ss.at[0], z_rs.at[chunk]
             ).start()
 
-    def send_corners(first, count, d):
-        part = pl.ds(first, count)
-        rows = pl.ds(ny - TILE if d == 0 else 0, TILE)
+    def pack_corners(part):
+        layers = (0,) if part == 0 else range(1, len(chunks))
+        for d in (0, 1):
+            first = ny - CORNER if d == 0 else 0
+            for z in (0, 1):
+                for n, chunk in enumerate(layers):
+                    zc[part, d, z, pl.ds(CORNER * n, CORNER), :] = zs[
+                        chunk, z, pl.ds(first, CORNER), :
+                    ]
+                rest = TILE - CORNER * len(layers)
+                zc[part, d, z, pl.ds(TILE - rest, rest), :] = jnp.zeros((rest, nz), jnp.float32)
+
+    def send_corners(part, d):
         for z in (0, 1):
             remote(
-                ((1, d), (2, z)), zs.at[part, z, rows], zd.at[d, part, z],
-                d_ss.at[0], d_rs.at[first // 2],
+                ((1, d), (2, z)), zc.at[part, d, z], zd.at[part, d, z],
+                d_ss.at[0], d_rs.at[part],
             ).start()
+
+    def wait_corners(part):
+        remote(
+            ((1, 0),), zd.at[part], zd.at[part], d_ss.at[0], d_rs.at[part]
+        ).wait_recv()
 
     def send_y(kind, d):
         _, start, size = yrows[kind]
@@ -390,10 +405,16 @@
             ((1, d),), ys.at[d, rows], yr.at[d, rows], y_ss.at[0], y_rs.at[kind]
         ).start()
 
-    def first_down():
-        await_ready(1, 1)
-        send_corners(0, 2, 1)
-        send_y(0, 1)
+    def first_rows(d):
+        await_ready(1, d)
+        send_corners(0, d)
+        send_y(0, d)
+
+    def bulk_down(kinds):
+        for kind in kinds:
+            send_y(kind, 1)
+        if 4 in kinds:
+            send_corners(1, 1)
 
     def early(m):
         v = SPEEDS[m][1]
@@ -478,9 +499,10 @@
         start, width = next((s, c) for k, at, s, c in zcols[chunk][z] if (k, at) == (m, x))
         count = abs(SPEEDS[m][1])
         shift = (start if z == 0 else start + width) % nz
-        tile = zd[d, chunk, z]
+        tile = zd[min(chunk, 1), d, z]
         moved = pltpu.roll(tile, nz - shift, 1) if shift else tile
-        moved = moved[TILE - count :] if d == 0 else moved[:count]
+        first = CORNER * max(chunk - 1, 0) + (CORNER - count if d == 0 else 0)
+        moved = moved[first : first + count]
         line = lane[:count]
         return jnp.where(line < width if z == 0 else line >= nz - width, moved, rows)
 
@@ -505,26 +527,37 @@
                 if x == order[0]:
                     await_ready(0)
                 send_edge(x)
+                if x == order[3]:
+                    wait(ready.at[4], source[0] + source[1])
+                    ferry_when(source, board)
 
             work(x, chunk, packed, between)
+            if chunk == 2 and n == 1:
+                pack_y(3)
+                send_y(3, 0)
+                pl.when(me[1] == 1)(lambda: bulk_down((3,)))
         for d in (0, 1):
             zs[chunk, d] = packed[d]
         if chunk == 0:
             await_ready(2)
         send_z(chunk)
+        if chunk == 0:
+            pack_y(1)
+            pl.when(last[0] == 1)(lambda: send_y(1, 0))
         if chunk == 1:
-            wait(ready.at[4], source[0] + source[1])
-            ferry_when(source, board)
+            pack_corners(0)
             pack_y(0)
-            pack_y(1)
-            await_ready(1, 0)
-            send_corners(0, 2, 0)
-            send_y(0, 0)
-            send_y(1, 0)
-            pl.when(above[1][1] == 0)(first_down)
-    pack_y(2)
-    send_y(2, 0)
-    send_corners(2, 1, 0)
+            pack_y(2)
+            first_rows(0)
+            pl.when(last[0] == 0)(lambda: send_y(1, 0))
+            send_y(2, 0)
+            pl.when(above[1][1] == 0)(lambda: first_rows(1))
+            pl.when(me[1] == 1)(lambda: bulk_down((1, 2)))
+    pack_y(4)
+    pack_corners(1)
+    send_y(4, 0)
+    send_corners(1, 0)
+    pl.when(me[1] == 1)(lambda: bulk_down((4,)))
 
     def wait_z(chunk):
         remote(((2, 0),), zs.at[chunk], zr.at[chunk], z_ss.at[0], z_rs.at[chunk]).wait_recv()
@@ -539,10 +572,8 @@
     for x in chunks[1]:
         send_tilted(x)
 
-    pl.when(above[1][1] == 1)(first_down)
-    send_y(1, 1)
-    send_y(2, 1)
-    send_corners(2, 1, 1)
+    pl.when(above[1][1] == 1)(lambda: first_rows(1))
+    pl.when(me[1] != 1)(lambda: bulk_down((1, 2, 3, 4)))
     settle_z(0, stays)
     settle_z(1, stays)
 
@@ -551,25 +582,20 @@
         part = (slice(None), pl.ds(first, size))
         remote(((1, 0),), ys.at[part], yr.at[part], y_ss.at[0], y_rs.at[kind]).wait_recv()
 
-    def wait_corners(first, count):
-        part = zd.at[:, pl.ds(first, count)]
-        remote(((1, 0),), part, part, d_ss.at[0], d_rs.at[first // 2]).wait_recv()
-
     wait_y(0)
     settle_y(0, lambda m, x: SPEEDS[m][2] == 0)
     for x in order:
         send_late(x, 0)
-    wait_corners(0, 2)
+    wait_corners(0)
     settle_y(0, lambda m, x: SPEEDS[m][2] != 0)
     for x in order:
         send_late(x, 1)
     wait_z(2)
     settle_z(2, stays)
-    wait_corners(2, 1)
-    wait_y(1)
-    settle_y(1, stays)
-    wait_y(2)
-    settle_y(2, stays)
+    wait_corners(1)
+    for kind in range(1, 5):
+        wait_y(kind)
+        settle_y(kind, stays)
     units = sum(abs(c[0]) for c in SPEEDS)
     layers = max(n for n in range(1, nx + 1) if units % n == 0)
     span = ext.at[pl.ds(0, units // layers), pl.ds(0, layers), pl.ds(PY, ny)]
@@ -578,7 +604,7 @@
     everything.wait_send()
     ferry_when(carrier, carried)
     remote(((1, 0),), ys, ys, y_ss.at[0], y_rs.at[0]).wait_send()
-    remote(((1, 0),), zd, zd, d_ss.at[0], d_rs.at[0]).wait_send()
+    remote(((1, 0),), zc, zd, d_ss.at[0], d_rs.at[0]).wait_send()
     remote(((2, 0),), zs, zs, z_ss.at[0], z_rs.at[0]).wait_send()
 
 
@@ -609,14 +635,15 @@
             pltpu.VMEM((nx, ny, nz), f32),
             pltpu.VMEM((3, 2, ny, nz), f32),
             pltpu.VMEM((3, 2, ny, nz), f32),
-            pltpu.VMEM((2, 3, 2, TILE, nz), f32),
+            pltpu.VMEM((2, 2, 2, TILE, nz), f32),
+            pltpu.VMEM((2, 2, 2, TILE, nz), f32),
             pltpu.VMEM((2, height, nz), f32),
             pltpu.VMEM((2, height, nz), f32),
             pltpu.VMEM((2, max(1, *FERRY), ny, nz), f32),
             dma((6,)),
             dma((1,)), dma((3,)),
             dma((1,)), dma((2,)),
-            dma((1,)), dma((3,)),
+            dma((1,)), dma((5,)),
             dma((1,)), dma((1,)),
             dma((2,)), dma((2,)),
             pltpu.SemaphoreType.REGULAR((5,)),

time: 16.5 us -> 15.9 us (0.964)
  Pallas kernels: 16.3 us -> 15.7 us
    pallas_call x1, Pallas kernels: 14.6 us -> 14 us  [per_device(): pl.pallas_call(kernel, out_shape=pltpu.VMEM(shape, f32), in_specs=[pl.Blo...]
where the time goes in v4:
time: 15.9 us; the launch traced here: 15.7 us
  Pallas kernels  15.7 us (99%)
    pallas_call x1, Pallas kernels, per_device(): pl.pallas_call(kernel, out_shape=pltpu.VMEM(shape, f32), in_specs=[pl.Blo...  14 us
    pallas_call x1, Pallas kernels, per_device(): pl.pallas_call(crop, out_shape=jax.ShapeDtypeStruct((Q, nx, ny, nz), f32)...  1.76 us

profile of v4, /device:TPU:0, one launch (start us, length us, event | category | flops | bytes accessed | tf_op | source)
XLA Modules:
  0.0 15.7 jit_solution(12481231264137936568)
XLA Ops:
  0.0 14.0 %shard_map.28.ext = f32[39,14,40,128]{3,2,1,0:T(8,128)S(1)} custom-call(f32[39,8,24,128]{3,2,1,0:T(8,128)} %pop.1, f32[8,24,128]{2,1,0:T(8,128)} %rate.1), custom_call_target="tpu_custom_call" | custom-call | tf_op jit(solution)/shard_map/pallas_call | solution.py:628
  14.0 1.8 %shard_map.29 = f32[39,8,24,128]{3,2,1,0:T(8,128)} custom-call(f32[39,14,40,128]{3,2,1,0:T(8,128)S(1)} %shard_map.28.ext), custom_call_target="tpu_custom_call" | custom-call | tf_op jit(solution)/shard_map/pallas_call | solution.py:655

commit v5 on v4

--- a/solution.py
+++ b/solution.py
@@ -67,6 +67,7 @@
     (m, o) for m, o in PAIRS if SPEEDS[m][2] == 0 and SPEEDS[m][0] != 0
 ]
 REST = [pair for pair in PAIRS if pair not in EDGE]
+PURE = [(m, o) for m, o in EDGE if SPEEDS[m][1] == 0]
 
 
 def crossing(m, x, nx):
@@ -214,18 +215,32 @@
 
 def kernel(
     pop, rate, ext, g, r, zs, zr, zc, zd, ys, yr, hop,
-    in_sem, z_ss, z_rs, d_ss, d_rs, y_ss, y_rs, x_ss, x_rs, h_ss, h_rs, ready,
+    in_sem, ss, z_rs, d_rs, y_rs, x_rs, h_ss, h_rs, ready,
 ):
     nx, ny, nz = pop.shape[1:]
     order, chunks, zcols, yrows, _ = plan(nx)
-    groups = [(x, 1) for x in order[:4]] + [(2, nx - 4)]
-    loads = [
-        pltpu.make_async_copy(
-            pop.at[:, pl.ds(first, count)], g.at[:, pl.ds(first, count)], in_sem.at[n]
-        )
-        for n, (first, count) in enumerate(groups)
+    head, tail = pl.ds(TILE, TILE), pl.ds(2 * TILE, ny - 2 * TILE)
+
+    def load(first, count, rows, n):
+        part = (slice(None), pl.ds(first, count), rows)
+        return pltpu.make_async_copy(pop.at[part], g.at[part], in_sem.at[n])
+
+    every = pl.ds(0, ny)
+    start_order = [
+        load(order[0], 1, head, 0),
+        pltpu.make_async_copy(rate, r, in_sem.at[1]),
+        load(order[0], 1, pl.ds(0, TILE), 2),
+        load(order[0], 1, tail, 2),
+        load(order[1], 1, every, 3),
+    ] + [load(x, 1, every, 4) for x in order[2:4]] + [load(2, nx - 4, every, 5)]
+    arrived = [
+        load(order[0], 1, head, 0),
+        pltpu.make_async_copy(rate, r, in_sem.at[1]),
+        load(order[0], 1, pl.ds(0, ny - TILE), 2),
+        load(order[1], 1, every, 3),
+        load(0, 2, every, 4),
+        load(2, nx - 4, every, 5),
     ]
-    loads.append(pltpu.make_async_copy(rate, r, in_sem.at[5]))
 
     around, above, nears = [], [], []
     for axis in AXES:
@@ -290,8 +305,8 @@
     for d in (0, 1):
         pl.when(source[d] == 1)(lambda: signal_to(barrier, beyond))
         pl.when(final == 1)(lambda d=d: signal_to(barrier, {**around[0][1 - d], **beyond}))
-    for n in (0, 5, 1, 2, 3, 4):
-        loads[n].start()
+    for copy in start_order:
+        copy.start()
     wait(
         barrier,
         sum(1 - is_above(steps) for steps, _ in links) + 2 * (carrier[0] + carrier[1]),
@@ -327,7 +342,7 @@
         which, rows = pl.ds(m, members), pl.ds(PY + rows[0], rows[1])
         return remote(
             ((0, d),), ext.at[which, pl.ds(at_x, 1), rows], ext.at[which, pl.ds(home, 1), rows],
-            x_ss.at[0], x_rs.at[0],
+            ss.at[0], x_rs.at[0],
         )
 
     def send_x(m, members, x, rows):
@@ -342,7 +357,7 @@
         for n, (m, x) in enumerate(ferry[d]):
             pltpu.make_async_remote_copy(
                 src_ref=ext.at[m, place(m, x), pl.ds(PY, ny)], dst_ref=hop.at[d, n],
-                send_sem=x_ss.at[0], recv_sem=h_rs.at[d],
+                send_sem=ss.at[0], recv_sem=h_rs.at[d],
                 device_id=beyond, device_id_type=MESH,
             ).start()
 
@@ -371,7 +386,7 @@
     def send_z(chunk):
         for d in (0, 1):
             remote(
-                ((2, d),), zs.at[chunk, d], zr.at[chunk, d], z_ss.at[0], z_rs.at[chunk]
+                ((2, d),), zs.at[chunk, d], zr.at[chunk, d], ss.at[0], z_rs.at[chunk]
             ).start()
 
     def pack_corners(part):
@@ -390,19 +405,19 @@
         for z in (0, 1):
             remote(
                 ((1, d), (2, z)), zc.at[part, d, z], zd.at[part, d, z],
-                d_ss.at[0], d_rs.at[part],
+                ss.at[0], d_rs.at[part],
             ).start()
 
     def wait_corners(part):
         remote(
-            ((1, 0),), zd.at[part], zd.at[part], d_ss.at[0], d_rs.at[part]
+            ((1, 0),), zd.at[part], zd.at[part], ss.at[0], d_rs.at[part]
         ).wait_recv()
 
     def send_y(kind, d):
         _, start, size = yrows[kind]
         rows = pl.ds(start, size)
         remote(
-            ((1, d),), ys.at[d, rows], yr.at[d, rows], y_ss.at[0], y_rs.at[kind]
+            ((1, d),), ys.at[d, rows], yr.at[d, rows], ss.at[0], y_rs.at[min(kind, 1)]
         ).start()
 
     def first_rows(d):
@@ -426,9 +441,27 @@
     def outgoing(x, chosen):
         return [m for m in range(Q) if crossing(m, x, nx) is not None and chosen(SPEEDS[m])]
 
+    def is_pure(m):
+        return SPEEDS[m][1] == 0 and SPEEDS[m][2] == 0
+
     def send_edge(x):
         for m in outgoing(x, lambda c: c[2] == 0):
-            send_x(m, 1, x, early(m))
+            if x == order[0] and is_pure(m):
+                send_x(m, 1, x, (0, TILE))
+                send_x(m, 1, x, (2 * TILE, ny - 2 * TILE))
+            else:
+                send_x(m, 1, x, early(m))
+
+    def first_tile(x):
+        def emit(m, value):
+            if crossing(m, x, nx) is not None:
+                ext[m, place(m, x), pl.ds(PY + TILE, TILE), :] = value
+
+        _, emit_pairs = collide(lambda m: g[m, x, head, :], r[x, head, :])
+        emit_pairs(PURE, emit)
+        await_ready(0)
+        for m in outgoing(x, lambda c: c[1] == 0 and c[2] == 0):
+            send_x(m, 1, x, (TILE, TILE))
 
     def send_tilted(x):
         for m in outgoing(x, lambda c: c[2] > 0):
@@ -451,6 +484,11 @@
                 mask = (lane >= start) & (lane < start + count)
                 packed[d] = jnp.where(mask, moved, packed[d])
                 value = pltpu.roll(value, cz % nz, 1)
+            if x == order[0] and is_pure(m) and crossing(m, x, nx) is not None:
+                for first, count in ((0, TILE), (2 * TILE, ny - 2 * TILE)):
+                    part = pl.ds(PY + first, count)
+                    ext[m, place(m, x), part, :] = value[first : first + count]
+                return
             ext[m, place(m, x), rows_at(m), :] = value
 
         emit_rest, emit_pairs = collide(lambda m: g[m, x], r[x])
@@ -458,6 +496,15 @@
         between()
         emit_rest(emit)
         emit_pairs(REST, emit)
+
+    def rows_view(count):
+        high, wide, deep = ext.shape[:3]
+        a, b, c = next(
+            (a, b, count // (a * b))
+            for a in range(high, 0, -1) for b in range(1, wide + 1)
+            if count % (a * b * TILE) == 0 and count // (a * b) <= deep
+        )
+        return ext.at[pl.ds(0, a), pl.ds(0, b), pl.ds(0, c)]
 
     def settle_z(chunk, chosen):
         for d in (0, 1):
@@ -516,16 +563,17 @@
     for chunk, layers in enumerate(chunks):
         packed = [blank, blank]
         for n, x in enumerate(layers):
-            if chunk < 2:
-                loads[2 * chunk + n].wait()
+            if x == order[0]:
+                arrived[0].wait()
+                arrived[1].wait()
+                first_tile(x)
+                arrived[2].wait()
+            elif x == order[1]:
+                arrived[3].wait()
             elif n == 0:
-                loads[4].wait()
-            if x == order[0]:
-                loads[5].wait()
+                arrived[chunk + 3].wait()
 
             def between(x=x):
-                if x == order[0]:
-                    await_ready(0)
                 send_edge(x)
                 if x == order[3]:
                     wait(ready.at[4], source[0] + source[1])
@@ -560,7 +608,7 @@
     pl.when(me[1] == 1)(lambda: bulk_down((4,)))
 
     def wait_z(chunk):
-        remote(((2, 0),), zs.at[chunk], zr.at[chunk], z_ss.at[0], z_rs.at[chunk]).wait_recv()
+        remote(((2, 0),), zs.at[chunk], zr.at[chunk], ss.at[0], z_rs.at[chunk]).wait_recv()
 
     ferry_when(carrier, carry)
     wait_z(0)
@@ -577,12 +625,14 @@
     settle_z(0, stays)
     settle_z(1, stays)
 
-    def wait_y(kind):
-        _, first, size = yrows[kind]
-        part = (slice(None), pl.ds(first, size))
-        remote(((1, 0),), ys.at[part], yr.at[part], y_ss.at[0], y_rs.at[kind]).wait_recv()
-
-    wait_y(0)
+    def wait_y(kinds):
+        first = yrows[kinds[0]][1]
+        part = (slice(None), pl.ds(first, sum(yrows[kind][2] for kind in kinds)))
+        remote(
+            ((1, 0),), ys.at[part], yr.at[part], ss.at[0], y_rs.at[min(kinds[0], 1)]
+        ).wait_recv()
+
+    wait_y((0,))
     settle_y(0, lambda m, x: SPEEDS[m][2] == 0)
     for x in order:
         send_late(x, 0)
@@ -593,19 +643,17 @@
     wait_z(2)
     settle_z(2, stays)
     wait_corners(1)
-    for kind in range(1, 5):
-        wait_y(kind)
+    bulk = tuple(range(1, len(yrows)))
+    wait_y(bulk)
+    for kind in bulk:
         settle_y(kind, stays)
     units = sum(abs(c[0]) for c in SPEEDS)
-    layers = max(n for n in range(1, nx + 1) if units % n == 0)
-    span = ext.at[pl.ds(0, units // layers), pl.ds(0, layers), pl.ds(PY, ny)]
-    everything = remote(((0, 0),), span, span, x_ss.at[0], x_rs.at[0])
-    everything.wait_recv()
-    everything.wait_send()
+    x_bytes = rows_view(units * ny)
+    remote(((0, 0),), x_bytes, x_bytes, ss.at[0], x_rs.at[0]).wait_recv()
+    total = units * ny + zs.shape[0] * 2 * ny + zc.shape[0] * 4 * TILE + 2 * ys.shape[1]
+    all_bytes = rows_view(total)
+    remote(((0, 0),), all_bytes, all_bytes, ss.at[0], x_rs.at[0]).wait_send()
     ferry_when(carrier, carried)
-    remote(((1, 0),), ys, ys, y_ss.at[0], y_rs.at[0]).wait_send()
-    remote(((1, 0),), zc, zd, d_ss.at[0], d_rs.at[0]).wait_send()
-    remote(((2, 0),), zs, zs, z_ss.at[0], z_rs.at[0]).wait_send()
 
 
 def crop(ext, out, sem):
@@ -641,10 +689,8 @@
             pltpu.VMEM((2, height, nz), f32),
             pltpu.VMEM((2, max(1, *FERRY), ny, nz), f32),
             dma((6,)),
-            dma((1,)), dma((3,)),
-            dma((1,)), dma((2,)),
-            dma((1,)), dma((5,)),
-            dma((1,)), dma((1,)),
+            dma((1,)),
+            dma((3,)), dma((2,)), dma((2,)), dma((1,)),
             dma((2,)), dma((2,)),
             pltpu.SemaphoreType.REGULAR((5,)),
         ],

time: 15.9 us -> 15.8 us (level)
  no operation moved by 1% of the time
where the time goes in v5:
time: 15.8 us; the launch traced here: 15.7 us
  Pallas kernels  15.7 us (99%)
    pallas_call x1, Pallas kernels, per_device(): pl.pallas_call(kernel, out_shape=pltpu.VMEM(shape, f32), in_specs=[pl.Blo...  13.9 us
    pallas_call x1, Pallas kernels, per_device(): pl.pallas_call(crop, out_shape=jax.ShapeDtypeStruct((Q, nx, ny, nz), f32)...  1.76 us

profile of v5, /device:TPU:0, one launch (start us, length us, event | category | flops | bytes accessed | tf_op | source)
XLA Modules:
  0.0 15.7 jit_solution(71490754464971800)
XLA Ops:
  0.0 13.9 %shard_map.28.ext = f32[39,14,40,128]{3,2,1,0:T(8,128)S(1)} custom-call(f32[39,8,24,128]{3,2,1,0:T(8,128)} %pop.1, f32[8,24,128]{2,1,0:T(8,128)} %rate.1), custom_call_target="tpu_custom_call" | custom-call | tf_op jit(solution)/shard_map/pallas_call | solution.py:676
  13.9 1.8 %shard_map.29 = f32[39,8,24,128]{3,2,1,0:T(8,128)} custom-call(f32[39,14,40,128]{3,2,1,0:T(8,128)S(1)} %shard_map.28.ext), custom_call_target="tpu_custom_call" | custom-call | tf_op jit(solution)/shard_map/pallas_call | solution.py:701

commit v6 on v5

--- a/solution.py
+++ b/solution.py
@@ -66,7 +66,10 @@
 EDGE = [
     (m, o) for m, o in PAIRS if SPEEDS[m][2] == 0 and SPEEDS[m][0] != 0
 ]
-REST = [pair for pair in PAIRS if pair not in EDGE]
+TILT = [
+    (m, o) for m, o in PAIRS if SPEEDS[m][2] != 0 and SPEEDS[m][0] != 0
+]
+OTHER = [pair for pair in PAIRS if pair not in EDGE + TILT]
 PURE = [(m, o) for m, o in EDGE if SPEEDS[m][1] == 0]
 
 
@@ -91,9 +94,13 @@
     for x in range((nx + 1) // 2):
         order += [x] if x == nx - 1 - x else [x, nx - 1 - x]
     chunks = [order[:2], order[2:4], order[4:]]
+    groups = [
+        (chunks[0], lambda m, x: crossing(m, x, nx) is not None),
+        (order[:4], lambda m, x: x not in order[:2] or crossing(m, x, nx) is None),
+        (order[4:], lambda m, x: True),
+    ]
     zcols = [
-        [slots(2, sign, layers, lambda m, x: True)[0] for sign in (1, -1)]
-        for layers in chunks
+        [slots(2, sign, layers, keep)[0] for sign in (1, -1)] for layers, keep in groups
     ]
     stages = chunks[:2] + [order[4:6], order[6:]]
     yrows, start = [], 0
@@ -422,7 +429,10 @@
 
     def first_rows(d):
         await_ready(1, d)
-        send_corners(0, d)
+        if d == 0:
+            pl.when(last[0] == 0)(lambda: send_corners(0, 0))
+        else:
+            send_corners(0, 1)
         send_y(0, d)
 
     def bulk_down(kinds):
@@ -471,18 +481,27 @@
         for m in outgoing(x, lambda c: c[1] != 0 and (c[2] > 0 if tilted else c[2] == 0)):
             send_x(m, 1 + tilted, x, late(m))
 
-    def work(x, chunk, packed, between):
-        slot = [{m: (s, c) for m, at, s, c in zcols[chunk][d] if at == x} for d in (0, 1)]
-
+    def group(m, x):
+        if x in chunks[0] and crossing(m, x, nx) is not None:
+            return 0
+        return 2 if x in chunks[2] else 1
+
+    slot = {
+        (m, x): (start, count)
+        for table in zcols for rows in table for m, x, start, count in rows
+    }
+
+    def store(x):
         def emit(m, value):
             cz = SPEEDS[m][2]
             if cz:
                 d = 0 if cz > 0 else 1
-                start, count = slot[d][m]
+                start, count = slot[m, x]
                 shift = (start + count if d == 0 else start) % nz
                 moved = pltpu.roll(value, shift, 1) if shift else value
                 mask = (lane >= start) & (lane < start + count)
-                packed[d] = jnp.where(mask, moved, packed[d])
+                mine = packed[group(m, x)]
+                mine[d] = jnp.where(mask, moved, mine[d])
                 value = pltpu.roll(value, cz % nz, 1)
             if x == order[0] and is_pure(m) and crossing(m, x, nx) is not None:
                 for first, count in ((0, TILE), (2 * TILE, ny - 2 * TILE)):
@@ -491,11 +510,10 @@
                 return
             ext[m, place(m, x), rows_at(m), :] = value
 
-        emit_rest, emit_pairs = collide(lambda m: g[m, x], r[x])
-        emit_pairs(EDGE, emit)
-        between()
-        emit_rest(emit)
-        emit_pairs(REST, emit)
+        return emit
+
+    def layer(x):
+        return collide(lambda m: g[m, x], r[x])
 
     def rows_view(count):
         high, wide, deep = ext.shape[:3]
@@ -542,8 +560,8 @@
                 ext[m, place(m, x), pl.ds(home, count), :] = rows
 
     def corner(d, z, m, x, rows):
-        chunk = next(n for n, layers in enumerate(chunks) if x in layers)
-        start, width = next((s, c) for k, at, s, c in zcols[chunk][z] if (k, at) == (m, x))
+        chunk = group(m, x)
+        start, width = slot[m, x]
         count = abs(SPEEDS[m][1])
         shift = (start if z == 0 else start + width) % nz
         tile = zd[min(chunk, 1), d, z]
@@ -560,61 +578,93 @@
         return crossing(m, x, nx) is None
 
     blank = jnp.zeros((ny, nz), jnp.float32)
-    for chunk, layers in enumerate(chunks):
-        packed = [blank, blank]
-        for n, x in enumerate(layers):
-            if x == order[0]:
-                arrived[0].wait()
-                arrived[1].wait()
-                first_tile(x)
-                arrived[2].wait()
-            elif x == order[1]:
-                arrived[3].wait()
-            elif n == 0:
-                arrived[chunk + 3].wait()
-
-            def between(x=x):
-                send_edge(x)
-                if x == order[3]:
-                    wait(ready.at[4], source[0] + source[1])
-                    ferry_when(source, board)
-
-            work(x, chunk, packed, between)
-            if chunk == 2 and n == 1:
-                pack_y(3)
-                send_y(3, 0)
-                pl.when(me[1] == 1)(lambda: bulk_down((3,)))
+    packed = [[blank, blank] for _ in chunks]
+
+    def wait_z(chunk):
+        remote(((2, 0),), zs.at[chunk], zr.at[chunk], ss.at[0], z_rs.at[chunk]).wait_recv()
+
+    carries = carrier[0] + carrier[1]
+
+    def tilted():
+        for x in chunks[0]:
+            send_tilted(x)
+
+    def flush(chunk):
         for d in (0, 1):
-            zs[chunk, d] = packed[d]
-        if chunk == 0:
-            await_ready(2)
-        send_z(chunk)
-        if chunk == 0:
-            pack_y(1)
-            pl.when(last[0] == 1)(lambda: send_y(1, 0))
-        if chunk == 1:
-            pack_corners(0)
-            pack_y(0)
-            pack_y(2)
-            first_rows(0)
-            pl.when(last[0] == 0)(lambda: send_y(1, 0))
-            send_y(2, 0)
-            pl.when(above[1][1] == 0)(lambda: first_rows(1))
-            pl.when(me[1] == 1)(lambda: bulk_down((1, 2)))
+            zs[chunk, d] = packed[chunk][d]
+        if chunk:
+            send_z(chunk)
+
+    def first_z():
+        await_ready(2)
+        send_z(0)
+
+    slow = apart[0] * above[2][0] + apart[1] * above[2][1]
+
+    for n, x in enumerate(chunks[0]):
+        if n == 0:
+            arrived[0].wait()
+            arrived[1].wait()
+            first_tile(x)
+        arrived[2 + n].wait()
+        _, emit_pairs = layer(x)
+        emit_pairs(EDGE, store(x))
+        send_edge(x)
+        emit_pairs(TILT, store(x))
+    flush(0)
+    pl.when(slow == 0)(first_z)
+    pack_corners(0)
+    pl.when(last[0] == 1)(lambda: send_corners(0, 0))
+    for x in chunks[0]:
+        emit_rest, emit_pairs = layer(x)
+        emit_rest(store(x))
+        emit_pairs(OTHER, store(x))
+    pl.when(slow > 0)(first_z)
+    pack_y(1)
+    pl.when(last[0] == 1)(lambda: send_y(1, 0))
+
+    def whole(x):
+        emit_rest, emit_pairs = layer(x)
+        emit_pairs(EDGE, store(x))
+        send_edge(x)
+        if x == order[3]:
+            wait(ready.at[4], source[0] + source[1])
+            ferry_when(source, board)
+        emit_pairs(TILT, store(x))
+        emit_rest(store(x))
+        emit_pairs(OTHER, store(x))
+
+    arrived[4].wait()
+    for x in chunks[1]:
+        whole(x)
+    flush(1)
+    pack_y(0)
+    pack_y(2)
+    first_rows(0)
+    pl.when(last[0] == 0)(lambda: send_y(1, 0))
+    send_y(2, 0)
+    pl.when(above[1][1] == 0)(lambda: first_rows(1))
+    pl.when(me[1] == 1)(lambda: bulk_down((1, 2)))
+    arrived[5].wait()
+    for n, x in enumerate(chunks[2]):
+        if n == 3:
+            wait_z(0)
+            settle_z(0, crosses)
+            pl.when(carries == 0)(tilted)
+        whole(x)
+        if n == 1:
+            pack_y(3)
+            send_y(3, 0)
+            pl.when(me[1] == 1)(lambda: bulk_down((3,)))
+    flush(2)
     pack_y(4)
     pack_corners(1)
     send_y(4, 0)
     send_corners(1, 0)
     pl.when(me[1] == 1)(lambda: bulk_down((4,)))
 
-    def wait_z(chunk):
-        remote(((2, 0),), zs.at[chunk], zr.at[chunk], ss.at[0], z_rs.at[chunk]).wait_recv()
-
     ferry_when(carrier, carry)
-    wait_z(0)
-    settle_z(0, crosses)
-    for x in chunks[0]:
-        send_tilted(x)
+    pl.when(carries > 0)(tilted)
     wait_z(1)
     settle_z(1, crosses)
     for x in chunks[1]:
@@ -622,7 +672,6 @@
 
     pl.when(above[1][1] == 1)(lambda: first_rows(1))
     pl.when(me[1] != 1)(lambda: bulk_down((1, 2, 3, 4)))
-    settle_z(0, stays)
     settle_z(1, stays)
 
     def wait_y(kinds):

time: 15.8 us -> 15.7 us (level)
  Pallas kernels: 15.7 us -> 15.5 us
where the time goes in v6:
time: 15.7 us; the launch traced here: 15.6 us
  Pallas kernels  15.5 us (99%)
    pallas_call x1, Pallas kernels, per_device(): pl.pallas_call(kernel, out_shape=pltpu.VMEM(shape, f32), in_specs=[pl.Blo...  13.8 us
    pallas_call x1, Pallas kernels, per_device(): pl.pallas_call(crop, out_shape=jax.ShapeDtypeStruct((Q, nx, ny, nz), f32)...  1.76 us

profile of v6, /device:TPU:0, one launch (start us, length us, event | category | flops | bytes accessed | tf_op | source)
XLA Modules:
  0.0 15.6 jit_solution(4203050240402974864)
XLA Ops:
  0.0 13.8 %shard_map.28.ext = f32[39,14,40,128]{3,2,1,0:T(8,128)S(1)} custom-call(f32[39,8,24,128]{3,2,1,0:T(8,128)} %pop.1, f32[8,24,128]{2,1,0:T(8,128)} %rate.1), custom_call_target="tpu_custom_call" | custom-call | tf_op jit(solution)/shard_map/pallas_call | solution.py:725
  13.8 1.8 %shard_map.29 = f32[39,8,24,128]{3,2,1,0:T(8,128)} custom-call(f32[39,14,40,128]{3,2,1,0:T(8,128)S(1)} %shard_map.28.ext), custom_call_target="tpu_custom_call" | custom-call | tf_op jit(solution)/shard_map/pallas_call | solution.py:750
